TPU v7x, 128 devices: a whole 4x4x4 slice. The times are simulated.
128 devices in a mesh: dp: 1, sp: 128 (over z, y, x, core).
Axes of the slice: x: 4, y: 4, z: 4, core: 2. Of those that a mesh axis runs over, the one named last changes fastest.
Arguments:
- x_in: bfloat16 [4096, 3584], P(('dp', 'sp'))
- seg_id: int32 [4096], P(('dp', 'sp'))
- pos_id: int32 [4096], P(('dp', 'sp'))
- w_dq: bfloat16 [3584, 768], replicated
- g_q: bfloat16 [768], replicated
- w_uq: bfloat16 [768, 24576], replicated
- w_dkv: bfloat16 [3584, 576], replicated
- g_kv: bfloat16 [512], replicated
- w_ukv: bfloat16 [512, 32768], replicated
- w_o: bfloat16 [16384, 3584], replicated
- g_ffn: bfloat16 [3584], replicated
- w_gate: bfloat16 [3584, 9216], P(None, 'sp')
- w_up: bfloat16 [3584, 9216], P(None, 'sp')
- w_down: bfloat16 [9216, 3584], P('sp')
Outputs:
- output: bfloat16 [4096, 3584], P(('dp', 'sp'))
All inputs are finite; a program needn't handle non-finite values.
Results may differ from a plain program's by a relative error of at most 0.0161625.
Values are sent between devices in bfloat16 or wider.
A program may use at most 1 GiB of HBM per device.

v0:
```python
import functools

import jax
import jax.numpy as jnp
from jax import lax
from jax.experimental import pallas as pl
from jax.experimental.pallas import tpu as pltpu
from jax.sharding import PartitionSpec as P

NOPE_DIM = 128
ROPE_DIM = 64
VALUE_DIM = 128
KV_LATENT = 512
QK_DIM = NOPE_DIM + ROPE_DIM
KV_DIM = NOPE_DIM + VALUE_DIM
SCORE_SCALE = QK_DIM ** -0.5
LOG2E = 1.4426950408889634
MASKED = -0.7 * 3.4028234663852886e38

RING = 4
CORES = 2


def rms_norm(vec_in, gain_vec):
    mean_sq = jnp.mean(vec_in * vec_in, axis=-1, keepdims=True)
    return vec_in * lax.rsqrt(mean_sq + 1e-6) * gain_vec.astype(jnp.float32)


def rope_angles(positions):
    half_dim = ROPE_DIM // 2
    inv_freq = 10000.0 ** (-jnp.arange(half_dim, dtype=jnp.float32) / half_dim)
    return positions.astype(jnp.float32)[..., None] * inv_freq


def apply_rope(vec_in, positions):
    half_dim = ROPE_DIM // 2
    angles = rope_angles(positions)
    cosine = jnp.cos(angles)
    sine_v = jnp.sin(angles)
    lo_half = vec_in[..., :half_dim]
    hi_half = vec_in[..., half_dim:]
    return jnp.concatenate([lo_half * cosine - hi_half * sine_v, hi_half * cosine + lo_half * sine_v], axis=-1)


GATHER_ORDERS = (("x", "y", "z"), ("y", "z", "x"), ("z", "x", "y"))


def gather_kernel_copies(bufs, coord, send_sem, recv_sem, fill_own):
    core = coord["core"]

    def device(**moved):
        c = {**coord, **moved}
        return {"sp": ((c["z"] * RING + c["y"]) * RING + c["x"]) * CORES + c["core"]}

    def step(axis, by):
        return lax.rem(coord[axis] + (by % RING), RING)

    up = {a: device(**{a: step(a, 1)}) for a in "xyz"}
    down = {a: device(**{a: step(a, -1)}) for a in "xyz"}
    partner = device(core=1 - core)

    barrier = pltpu.get_barrier_semaphore()
    for nb in list(up.values()) + list(down.values()) + [partner]:
        pl.semaphore_signal(barrier, inc=1, device_id=nb, device_id_type=pl.DeviceIdType.MESH)
    fill_own()
    pl.semaphore_wait(barrier, 7)

    copies = [{} for _ in bufs]

    def send(p, key, dev, rows=None, **at):
        idx = tuple(slice(None) if at.get(a, 0) is None else at.get(a, coord[a]) for a in "zyx") + (core,)
        if rows is not None:
            idx = idx + (rows,)
        n = len(copies[p])
        cp = pltpu.make_async_remote_copy(
            src_ref=bufs[p].at[idx], dst_ref=bufs[p].at[idx], send_sem=send_sem.at[p, n], recv_sem=recv_sem.at[p, n],
            device_id=dev, device_id_type=pl.DeviceIdType.MESH)
        cp.start()
        copies[p][key] = cp

    n_p = len(bufs)
    pieces = range(n_p)
    half = bufs[0].shape[4] // 2
    order = (0, -1, 1, 2)

    def along_b(p, da):
        a, b, _ = GATHER_ORDERS[p]
        send(p, ("b+", da), up[b], **{a: step(a, da)})
        send(p, ("b-", da), down[b], **{a: step(a, da)})

    def along_d(p, db):
        a, b, d = GATHER_ORDERS[p]
        send(p, ("d+", db), up[d], **{a: None, b: step(b, db)})
        send(p, ("d-", db), down[d], **{a: None, b: step(b, db)})
        to_partner(p, db, 0)

    def to_partner(p, db, dd):
        a, b, d = GATHER_ORDERS[p]
        send(p, ("p", db, dd), partner, **{a: None, b: step(b, db), d: step(d, dd)})

    for p in pieces:
        a, b, d = GATHER_ORDERS[p]
        send(p, "a+", up[a])
        send(p, "a-", down[a])
        along_b(p, 0)
    for p in pieces:
        a, b, d = GATHER_ORDERS[p]
        copies[p]["a+"].wait_recv()
        send(p, "af+", up[a], rows=slice(0, half), **{a: step(a, -1)})
        copies[p]["a-"].wait_recv()
        send(p, "af-", down[a], rows=slice(half, 2 * half), **{a: step(a, 1)})
        along_b(p, -1)
        along_b(p, 1)
    for p in pieces:
        copies[p]["af+"].wait_recv()
        copies[p]["af-"].wait_recv()
        along_b(p, 2)
        along_d(p, 0)
    for p in pieces:
        a, b, d = GATHER_ORDERS[p]
        for da in (0, -1):
            copies[p][("b+", da)].wait_recv()
            send(p, ("bf+", da), up[b], **{a: step(a, da), b: step(b, -1)})
        for da in (1, 2):
            copies[p][("b-", da)].wait_recv()
            send(p, ("bf-", da), down[b], **{a: step(a, da), b: step(b, 1)})
        for da in (1, 2):
            copies[p][("b+", da)].wait_recv()
        along_d(p, -1)
        for da in (0, -1):
            copies[p][("b-", da)].wait_recv()
        along_d(p, 1)
    for p in pieces:
        for da in (0, -1):
            copies[p][("bf+", da)].wait_recv()
        for da in (1, 2):
            copies[p][("bf-", da)].wait_recv()
        along_d(p, 2)
    for db in order:
        for p in pieces:
            a, b, d = GATHER_ORDERS[p]
            copies[p][("d+", db)].wait_recv()
            if db in (0, -1):
                send(p, ("df+", db), up[d], **{a: None, b: step(b, db), d: step(d, -1)})
            to_partner(p, db, -1)
            copies[p][("d-", db)].wait_recv()
            if db in (1, 2):
                send(p, ("df-", db), down[d], **{a: None, b: step(b, db), d: step(d, 1)})
            to_partner(p, db, 1)
    for db in order:
        for p in pieces:
            copies[p][("df+" if db in (0, -1) else "df-", db)].wait_recv()
            to_partner(p, db, 2)
    for p in pieces:
        for db in order:
            for dd in order:
                copies[p][("p", db, dd)].wait_recv()
    for p in pieces:
        for cp in copies[p].values():
            cp.wait_send()


GATHER_COPIES = 44


def my_coord():
    me = lax.axis_index("sp")
    return {
        "core": lax.rem(me, CORES),
        "x": lax.rem(me // CORES, RING),
        "y": lax.rem(me // (CORES * RING), RING),
        "z": me // (CORES * RING * RING),
    }


def qkv_kernel(kv_own, qa_own, qb_own, wqa, wqb, wk, wv, inv_freq, pick, qt_out, k_out, vt_out, pos_out,
               kv_buf, qa_buf, qb_buf, send_sem, recv_sem, *, blk):
    coord = my_coord()

    def fill_own():
        at = (coord["z"], coord["y"], coord["x"], coord["core"])
        kv_buf[at] = kv_own[...]
        qa_buf[at] = qa_own[...]
        qb_buf[at] = qb_own[...]

    gather_kernel_copies((kv_buf, qa_buf, qb_buf), coord, send_sem, recv_sem, fill_own)

    nt = (((1,), (1,)), ((), ()))
    half = ROPE_DIM // 2
    tok_blk = kv_own.shape[0]
    shards = blk // tok_blk
    lines = shards // (RING * CORES)
    n_blk = qt_out.shape[1] // blk
    per_z = RING // lines
    f32, bf16 = jnp.float32, jnp.bfloat16

    @pl.loop(0, n_blk)
    def _(n):
        at = (n // per_z, pl.ds(lax.rem(n, per_z) * lines, lines))
        flat = lambda v: v.reshape(blk, v.shape[-1])
        lat = flat(kv_buf[at])
        qa = flat(qa_buf[at])
        qb = flat(qb_buf[at])
        tail = qb[:, qb.shape[1] - NOPE_DIM:]
        rows = pl.ds(pl.multiple_of(n * blk, blk), blk)
        k_out[rows, :NOPE_DIM] = jnp.dot(lat, wk[...], preferred_element_type=f32).astype(bf16)
        k_out[rows, NOPE_DIM:] = tail
        vt_out[:, rows] = lax.dot_general(wv[...], lat, nt, preferred_element_type=f32).astype(bf16)
        pos = lax.dot_general(pick[...], tail, nt, preferred_element_type=f32)
        pos_out[:, rows] = pos
        angle = inv_freq[...] * pos[0:1]
        cosine, sine = jnp.cos(angle), jnp.sin(angle)
        qt = lax.dot_general(wqa[...], qa, nt, preferred_element_type=f32)
        qt += lax.dot_general(wqb[...], qb[:, :qb.shape[1] - NOPE_DIM], nt, preferred_element_type=f32)
        lo, hi = qt[NOPE_DIM:NOPE_DIM + half], qt[NOPE_DIM + half:]
        qt_out[:NOPE_DIM, rows] = qt[:NOPE_DIM].astype(bf16)
        qt_out[NOPE_DIM:NOPE_DIM + half, rows] = (lo * cosine - hi * sine).astype(bf16)
        qt_out[NOPE_DIM + half:QK_DIM, rows] = (hi * cosine + lo * sine).astype(bf16)
        qt_out[QK_DIM:, rows] = jnp.zeros((2 * NOPE_DIM - QK_DIM, blk), bf16)


def gather_qkv(kv_own, qa_own, qb_own, w_uq, w_ukv, tok_total, blk):
    rows = kv_own.shape[0]
    f32, bf16 = jnp.float32, jnp.bfloat16
    half = ROPE_DIM // 2
    inv_freq = 10000.0 ** (-jnp.arange(half, dtype=f32) / half)
    lane = jnp.arange(NOPE_DIM)[None, :]
    pick = jnp.where(jnp.arange(8)[:, None] == 0, jnp.where(lane == ROPE_DIM, 64.0, jnp.where(lane == ROPE_DIM + 1, 1.0, 0.0)), 0.0).astype(bf16)
    vm = pl.BlockSpec(memory_space=pltpu.VMEM)
    wa = qa_own.shape[1]
    buf = lambda own: pltpu.VMEM((RING, RING, RING, CORES, rows, own.shape[1]), bf16)
    return pl.pallas_call(
        functools.partial(qkv_kernel, blk=blk),
        name="gather_qkv",
        out_shape=(
            jax.ShapeDtypeStruct((2 * NOPE_DIM, tok_total), bf16),
            jax.ShapeDtypeStruct((tok_total, 2 * NOPE_DIM), bf16),
            jax.ShapeDtypeStruct((VALUE_DIM, tok_total), bf16),
            jax.ShapeDtypeStruct((8, tok_total), f32),
        ),
        in_specs=[vm] * 9,
        out_specs=(vm,) * 4,
        scratch_shapes=[
            buf(kv_own), buf(qa_own), buf(qb_own),
            pltpu.SemaphoreType.DMA((3, GATHER_COPIES)),
            pltpu.SemaphoreType.DMA((3, GATHER_COPIES)),
        ],
        cost_estimate=pl.CostEstimate(flops=4_000_000_000, bytes_accessed=6_000_000, transcendentals=0),
        compiler_params=pltpu.CompilerParams(collective_id=2, has_side_effects=True, vmem_limit_bytes=40 << 20),
    )(kv_own, qa_own, qb_own, w_uq[:wa].T, w_uq[wa:].T, w_ukv[:, :NOPE_DIM], w_ukv[:, NOPE_DIM:].T, inv_freq[:, None], pick)


def attn_kernel(lo_ref, clear_ref, q_ref, k_ref, v_ref, start_ref, pos_ref, o_ref, acc_ref, *, blk):
    i = pl.program_id(0)
    acc_ref[...] = jnp.zeros_like(acc_ref)

    def block(masked, kb, carry):
        m_old, l_old = carry
        rows = pl.ds(pl.multiple_of(kb * blk, blk), blk)
        s = jnp.dot(k_ref[rows, :], q_ref[...], preferred_element_type=jnp.float32)
        if masked:
            key = kb * blk + lax.broadcasted_iota(jnp.int32, s.shape, 0)
            back = key - start_ref[...]
            s = jnp.where((back >= 0) & (back <= pos_ref[...]), s, MASKED)
        m_new = jnp.maximum(m_old, jnp.max(s, axis=0, keepdims=True))
        p = jnp.exp2((s - m_new) * (SCORE_SCALE * LOG2E))
        alpha = jnp.exp2((m_old - m_new) * (SCORE_SCALE * LOG2E))
        l_new = l_old * alpha + jnp.sum(p, axis=0, keepdims=True)
        acc_ref[...] = acc_ref[...] * alpha + jnp.dot(v_ref[:, rows], p.astype(jnp.bfloat16), preferred_element_type=jnp.float32)
        return m_new, l_new

    carry = (jnp.full((1, blk), MASKED, jnp.float32), jnp.zeros((1, blk), jnp.float32))
    lo = lo_ref[i]
    clear = clear_ref[i]
    carry = lax.fori_loop(lo, clear, functools.partial(block, True), carry)
    carry = lax.fori_loop(clear, i, functools.partial(block, False), carry)
    _, total = block(True, i, carry)
    o_ref[...] = (acc_ref[...] / total).T.astype(jnp.bfloat16)


def attention(qt, k, vt, pos_row, blk):
    tok = k.shape[0]
    n_blk = tok // blk
    pos_all = pos_row.astype(jnp.int32)
    start = jnp.arange(tok, dtype=jnp.int32)[None, :] - pos_all
    lo = start[0, ::blk] // blk
    clear = jnp.clip((start[0, blk - 1::blk] + blk - 1) // blk, lo, jnp.arange(n_blk, dtype=jnp.int32))
    whole = lambda a: pl.BlockSpec(a.shape, lambda i, *_: (0, 0), pipeline_mode=pl.Buffered(1))
    lane_blk = lambda r: pl.BlockSpec((r, blk), lambda i, *_: (0, i))
    return pl.pallas_call(
        functools.partial(attn_kernel, blk=blk),
        name="attention",
        out_shape=jax.ShapeDtypeStruct((tok, VALUE_DIM), jnp.bfloat16),
        grid_spec=pltpu.PrefetchScalarGridSpec(
            num_scalar_prefetch=2,
            grid=(n_blk,),
            in_specs=[lane_blk(2 * NOPE_DIM), whole(k), whole(vt), lane_blk(1), lane_blk(1)],
            out_specs=pl.BlockSpec((blk, VALUE_DIM), lambda i, *_: (i, 0)),
            scratch_shapes=[pltpu.VMEM((VALUE_DIM, blk), jnp.float32)],
        ),
        cost_estimate=pl.CostEstimate(flops=10_000_000_000, bytes_accessed=8_000_000, transcendentals=9_000_000),
        compiler_params=pltpu.CompilerParams(dimension_semantics=("arbitrary",), vmem_limit_bytes=40 << 20),
    )(lo, clear, qt, k, vt, start, pos_all)


def project_kernel(o_ref, wo_ref, y_ref, o_all, w_buf, acc, y_half, y_in, w_sem, send_sem, recv_sem, fwd_send, fwd_recv,
                   y_sem, *, n_buf):
    coord = my_coord()
    core, x, y, z = (coord[a] for a in ("core", "x", "y", "z"))
    lines = RING * RING
    chip_rows, head = o_all.shape[3], o_all.shape[4]
    w_rows, cols = w_buf.shape[1], w_buf.shape[2]
    mesh_id = pl.DeviceIdType.MESH

    def line_of(k):
        return lax.rem(z + k // RING, RING) * RING + lax.rem(y + lax.rem(k, RING), RING)

    def w_copy(k):
        rows = pl.ds(pl.multiple_of(line_of(k) * w_rows, w_rows), w_rows)
        side = pl.ds(pl.multiple_of(core * cols, 128), cols)
        slot = lax.rem(k, n_buf)
        return pltpu.make_async_copy(wo_ref.at[rows, side], w_buf.at[slot], w_sem.at[slot])

    @pl.loop(0, n_buf)
    def _(k):
        w_copy(k).start()

    def chip(k, dx):
        zz = lax.rem(z + RING - k // RING, RING)
        yy = lax.rem(y + RING - lax.rem(k, RING), RING)
        xx = lax.rem(x + RING - dx, RING)
        return (zz * RING + yy) * RING + xx

    me_chip = (z * RING + y) * RING + x
    partner = {"sp": me_chip * CORES + 1 - core}
    n_chips = lines * RING

    barrier = pltpu.get_barrier_semaphore()
    pl.semaphore_signal(barrier, inc=1, device_id=partner, device_id_type=mesh_id)

    @pl.loop(1, n_chips)
    def _(n):
        to = {"sp": chip(n // RING, lax.rem(n, RING)) * CORES + core}
        pl.semaphore_signal(barrier, inc=1, device_id=to, device_id_type=mesh_id)

    my_line = z * RING + y
    o_all[my_line, x, core] = o_ref[pl.ds(pl.multiple_of(me_chip * chip_rows, chip_rows), chip_rows), :]
    pl.semaphore_wait(barrier, n_chips)

    def head_copy(n):
        to = chip(n // RING, lax.rem(n, RING))
        rows = pl.ds(pl.multiple_of(to * chip_rows, chip_rows), chip_rows)
        return pltpu.make_async_remote_copy(
            src_ref=o_ref.at[rows, :], dst_ref=o_all.at[my_line, x, core], send_sem=send_sem, recv_sem=recv_sem.at[n // RING],
            device_id={"sp": to * CORES + core}, device_id_type=mesh_id)

    @pl.loop(1, n_chips)
    def _(n):
        head_copy(n).start()

    def forward(k):
        at = o_all.at[line_of(k), :, core]
        return pltpu.make_async_remote_copy(
            src_ref=at, dst_ref=at, send_sem=fwd_send.at[k], recv_sem=fwd_recv.at[k], device_id=partner, device_id_type=mesh_id)

    def arrive(k, n_heads):
        at = o_all.at[line_of(k), pl.ds(0, n_heads), core]
        pltpu.make_async_copy(at, at, recv_sem.at[k]).wait()
        forward(k).start()

    acc[...] = jnp.zeros_like(acc)
    arrive(0, RING - 1)

    @pl.loop(0, lines)
    def _(k):
        @pl.when(k + 1 < lines)
        def _():
            arrive(k + 1, RING)

        forward(k).wait_recv()
        w_copy(k).wait()
        line = line_of(k)
        lhs = jnp.concatenate([o_all[line, i, j] for i in range(RING) for j in range(CORES)], axis=1)
        acc[...] += jnp.dot(lhs, w_buf[lax.rem(k, n_buf)], preferred_element_type=jnp.float32)

        @pl.when(k + n_buf < lines)
        def _():
            w_copy(k + n_buf).start()

    own_rows = chip_rows // CORES
    y_half[...] = acc[...].astype(jnp.bfloat16)
    swap = pltpu.make_async_remote_copy(
        src_ref=y_half.at[pl.ds(pl.multiple_of((1 - core) * own_rows, own_rows), own_rows), :], dst_ref=y_in,
        send_sem=y_sem.at[0], recv_sem=y_sem.at[1], device_id=partner, device_id_type=mesh_id)
    swap.start()
    mine = y_half[pl.ds(pl.multiple_of(core * own_rows, own_rows), own_rows), :]
    swap.wait_recv()
    other = y_in[...]
    y_ref[:, :cols] = jnp.where(core == 0, mine, other)
    y_ref[:, cols:] = jnp.where(core == 0, other, mine)
    swap.wait_send()

    @pl.loop(0, lines)
    def _(k):
        forward(k).wait_send()

    everything = o_ref.at[pl.ds(0, (n_chips - 1) * chip_rows), :]
    pltpu.make_async_copy(everything, everything, send_sem).wait()


def project(o_loc, w_o, group_size, n_buf):
    tok, head = o_loc.shape
    own_rows = tok // group_size
    dim = w_o.shape[1]
    lines = RING * RING
    w_rows = w_o.shape[0] // lines
    f32, bf16 = jnp.float32, jnp.bfloat16
    vm = pl.BlockSpec(memory_space=pltpu.VMEM)
    return pl.pallas_call(
        functools.partial(project_kernel, n_buf=n_buf),
        name="project",
        out_shape=jax.ShapeDtypeStruct((own_rows, dim), bf16),
        in_specs=[vm, pl.BlockSpec(memory_space=pl.ANY)],
        out_specs=vm,
        scratch_shapes=[
            pltpu.VMEM((lines, RING, CORES, CORES * own_rows, head), bf16),
            pltpu.VMEM((n_buf, w_rows, dim // CORES), bf16),
            pltpu.VMEM((CORES * own_rows, dim // CORES), f32),
            pltpu.VMEM((CORES * own_rows, dim // CORES), bf16),
            pltpu.VMEM((own_rows, dim // CORES), bf16),
            pltpu.SemaphoreType.DMA((n_buf,)),
            pltpu.SemaphoreType.DMA,
            pltpu.SemaphoreType.DMA((lines,)),
            pltpu.SemaphoreType.DMA((lines,)),
            pltpu.SemaphoreType.DMA((lines,)),
            pltpu.SemaphoreType.DMA((2,)),
        ],
        cost_estimate=pl.CostEstimate(flops=4_000_000_000, bytes_accessed=60_000_000, transcendentals=0),
        compiler_params=pltpu.CompilerParams(collective_id=3, has_side_effects=True, vmem_limit_bytes=56 << 20),
    )(o_loc, w_o)


def ffn_kernel(y_ref, g_ref, *rest, dim, pad, sub, tile_n):
    n_wt = 10
    weights = rest[:n_wt]
    (out_ref, ybuf, wgu, wdn, hbuf, gubuf, part, far_l, far_r, in_l, in_r, far2_l, far2_r, in2_l, in2_r,
     w_sem, ag_send, ag_recv, rs_send, rs_recv) = rest[n_wt:]
    me = lax.axis_index("sp")
    core = lax.rem(me, CORES)
    x = lax.rem(me // CORES, RING)
    y = lax.rem(me // (CORES * RING), RING)
    z = me // (CORES * RING * RING)

    def device(yy, xx):
        return {"sp": ((z * RING + yy) * RING + xx) * CORES + core}

    x_up, x_dn = device(y, lax.rem(x + 1, RING)), device(y, lax.rem(x + RING - 1, RING))
    y_up, y_dn = device(lax.rem(y + 1, RING), x), device(lax.rem(y + RING - 1, RING), x)
    up1, dn1, up2, dn2 = (x_up, y_up), (x_dn, y_dn), (y_up, x_up), (y_dn, x_dn)

    barrier = pltpu.get_barrier_semaphore()
    for nb in (x_up, x_dn, y_up, y_dn):
        pl.semaphore_signal(barrier, inc=1, device_id=nb, device_id_type=pl.DeviceIdType.MESH)

    w_copies = []

    def fetch(src, dst):
        cp = pltpu.make_async_copy(src, dst, w_sem.at[len(w_copies)])
        cp.start()
        w_copies.append(cp)

    cut = weights[3].shape[0]
    for side in range(2):
        own, left, right, f0, f1 = weights[5 * side:5 * side + 5]
        for n, blk in enumerate((own, left, right)):
            r = (4 * side + n) * pad
            fetch(blk.at[0:pad], wgu.at[r:r + pad])
            fetch(blk.at[pad:2 * pad], wgu.at[8 * pad + r:8 * pad + r + pad])
            fetch(blk.at[2 * pad:], wdn.at[r:r + pad])
        r = (4 * side + 3) * pad
        fetch(f0.at[0:pad], wgu.at[r:r + pad])
        fetch(f0.at[pad:cut], wgu.at[8 * pad + r:8 * pad + r + cut - pad])
        fetch(f1.at[0:2 * pad - cut], wgu.at[8 * pad + r + cut - pad:8 * pad + r + pad])
        fetch(f1.at[2 * pad - cut:], wdn.at[r:r + pad])

    for h in range(2):
        ybuf[h, 0] = y_ref[h * sub:(h + 1) * sub, :]
    pl.semaphore_wait(barrier, 4)

    cols = (slice(0, dim // 2), slice(dim // 2, dim))
    ag_copies = {}
    ag_n = [0]

    def ag_send_to(h, src_slot, dst_slot, dev, col=None):
        c = slice(None) if col is None else cols[col]
        key = (h, dst_slot, col)
        rsem = dst_slot if col != 1 else RING * RING
        cp = pltpu.make_async_remote_copy(
            src_ref=ybuf.at[h, src_slot, :, c], dst_ref=ybuf.at[h, dst_slot, :, c],
            send_sem=ag_send.at[ag_n[0]], recv_sem=ag_recv.at[h, rsem],
            device_id=dev, device_id_type=pl.DeviceIdType.MESH)
        ag_n[0] += 1
        cp.start()
        ag_copies[key] = cp

    far = 2
    for h in range(2):
        ag_send_to(h, 0, 3 * RING, up1[h])
        ag_send_to(h, 0, 1 * RING, dn1[h])
    for h in range(2):
        ag_send_to(h, 0, 3, up2[h])
        ag_send_to(h, 0, 1, dn2[h])
    for h in range(2):
        ag_copies[(h, 3 * RING, None)].wait_recv()
        ag_send_to(h, 3 * RING, far * RING, up1[h], 0)
        ag_copies[(h, 1 * RING, None)].wait_recv()
        ag_send_to(h, 1 * RING, far * RING, dn1[h], 1)
        for d1 in (3, 1):
            ag_send_to(h, d1 * RING, d1 * RING + 3, up2[h])
            ag_send_to(h, d1 * RING, d1 * RING + 1, dn2[h])
    for h in range(2):
        ag_copies[(h, far * RING, 0)].wait_recv()
        ag_copies[(h, far * RING, 1)].wait_recv()
        ag_send_to(h, far * RING, far * RING + 3, up2[h])
        ag_send_to(h, far * RING, far * RING + 1, dn2[h])
    for d1, d2, dev in ((0, 3, up2), (3, 3, up2), (1, 1, dn2), (2, 1, dn2)):
        for h in range(2):
            ag_copies[(h, d1 * RING + d2, None)].wait_recv()
            ag_send_to(h, d1 * RING + d2, d1 * RING + far, dev[h])
    for d1, d2 in ((0, 1), (3, 1), (1, 3), (2, 3), (0, 2), (3, 2), (1, 2), (2, 2)):
        for h in range(2):
            ag_copies[(h, d1 * RING + d2, None)].wait_recv()

    for cp in w_copies:
        cp.wait()

    rows = 2 * RING * sub
    nt = (((1,), (1,)), ((), ()))
    ff_pad = 8 * pad

    def compute(d1):
        for h in range(2):
            for d2 in range(RING):
                v = ybuf[h, d1 * RING + d2].astype(jnp.float32)
                mean_sq = jnp.mean(v * v, axis=-1, keepdims=True)
                r = (h * RING + d2) * sub
                hbuf[r:r + sub, :] = (v * lax.rsqrt(mean_sq + 1e-6) * g_ref[...].astype(jnp.float32)).astype(jnp.bfloat16)
        n_gu = gubuf.shape[1] // tile_n

        @pl.loop(0, n_gu)
        def _(j):
            c = pl.ds(pl.multiple_of(j * tile_n, tile_n), tile_n)
            gubuf[:, c] = lax.dot_general(hbuf[...], wgu[c, :], nt, preferred_element_type=jnp.float32)

        gate = gubuf[:, :ff_pad]
        act = (gate * jax.nn.sigmoid(gate) * gubuf[:, ff_pad:]).astype(jnp.bfloat16)
        wide = dim // 7 if dim % (7 * 128) == 0 else dim
        for j in range(dim // wide):
            c = slice(j * wide, (j + 1) * wide)
            res = jnp.dot(act, wdn[:, c], preferred_element_type=jnp.float32)
            for h in range(2):
                for d2 in range(RING):
                    r = (h * RING + d2) * sub
                    part[h, d1 * RING + d2, :, c] = res[r:r + sub]

    rs_copies = {}
    rs_n = [0]

    def rs_send_to(key, src, dst, dev):
        cp = pltpu.make_async_remote_copy(
            src_ref=src, dst_ref=dst, send_sem=rs_send.at[rs_n[0]], recv_sem=rs_recv.at[rs_n[0]],
            device_id=dev, device_id_type=pl.DeviceIdType.MESH)
        rs_n[0] += 1
        cp.start()
        rs_copies[key] = cp

    order = (2, 1, 3, 0)
    compute(far)
    for d2 in order:
        for h in range(2):
            rs_send_to(("fl", h, d2), part.at[h, far * RING + d2, :, cols[0]], far_l.at[h, d2], up1[h])
            rs_send_to(("fr", h, d2), part.at[h, far * RING + d2, :, cols[1]], far_r.at[h, d2], dn1[h])
    compute(1)
    compute(3)
    for d2 in order:
        for h in range(2):
            rs_copies[("fl", h, d2)].wait_recv()
            part[h, RING + d2, :, cols[0]] += far_l[h, d2]
            rs_send_to(("il", h, d2), part.at[h, RING + d2], in_l.at[h, d2], up1[h])
            rs_copies[("fr", h, d2)].wait_recv()
            part[h, 3 * RING + d2, :, cols[1]] += far_r[h, d2]
            rs_send_to(("ir", h, d2), part.at[h, 3 * RING + d2], in_r.at[h, d2], dn1[h])
    compute(0)

    def first_sum(h, d2):
        rs_copies[("il", h, d2)].wait_recv()
        rs_copies[("ir", h, d2)].wait_recv()
        part[h, d2] = part[h, d2] + in_l[h, d2] + in_r[h, d2]

    for h in range(2):
        first_sum(h, 2)
        rs_send_to(("gl", h), part.at[h, 2, :, cols[0]], far2_l.at[h], up2[h])
        rs_send_to(("gr", h), part.at[h, 2, :, cols[1]], far2_r.at[h], dn2[h])
    for h in range(2):
        first_sum(h, 1)
        rs_copies[("gl", h)].wait_recv()
        part[h, 1, :, cols[0]] += far2_l[h]
        rs_send_to(("jl", h), part.at[h, 1], in2_l.at[h], up2[h])
        first_sum(h, 3)
        rs_copies[("gr", h)].wait_recv()
        part[h, 3, :, cols[1]] += far2_r[h]
        rs_send_to(("jr", h), part.at[h, 3], in2_r.at[h], dn2[h])
    for h in range(2):
        first_sum(h, 0)
        rs_copies[("jl", h)].wait_recv()
        rs_copies[("jr", h)].wait_recv()
        total = part[h, 0] + in2_l[h] + in2_r[h]
        out_ref[h * sub:(h + 1) * sub, :] = (ybuf[h, 0].astype(jnp.float32) + total).astype(jnp.bfloat16)
    for cp in list(ag_copies.values()) + list(rs_copies.values()):
        cp.wait_send()


def ffn(y_own, g_ffn, weights, pad):
    rows, dim = y_own.shape
    sub = rows // 2
    chunk = 2 * RING * sub
    f32, bf16 = jnp.float32, jnp.bfloat16
    vm = pl.BlockSpec(memory_space=pltpu.VMEM)
    hbm = pl.BlockSpec(memory_space=pl.ANY)
    half = dim // 2
    return pl.pallas_call(
        functools.partial(ffn_kernel, dim=dim, pad=pad, sub=sub, tile_n=256 if (16 * pad) % 256 == 0 else 16 * pad),
        name="ffn",
        out_shape=jax.ShapeDtypeStruct((rows, dim), bf16),
        in_specs=[vm, vm] + [hbm] * 10,
        out_specs=vm,
        scratch_shapes=[
            pltpu.VMEM((2, RING * RING, sub, dim), bf16),
            pltpu.VMEM((16 * pad, dim), bf16),
            pltpu.VMEM((8 * pad, dim), bf16),
            pltpu.VMEM((chunk, dim), bf16),
            pltpu.VMEM((chunk, 16 * pad), f32),
            pltpu.VMEM((2, RING * RING, sub, dim), f32),
            pltpu.VMEM((2, RING, sub, half), f32),
            pltpu.VMEM((2, RING, sub, half), f32),
            pltpu.VMEM((2, RING, sub, dim), f32),
            pltpu.VMEM((2, RING, sub, dim), f32),
            pltpu.VMEM((2, sub, half), f32),
            pltpu.VMEM((2, sub, half), f32),
            pltpu.VMEM((2, sub, dim), f32),
            pltpu.VMEM((2, sub, dim), f32),
            pltpu.SemaphoreType.DMA((26,)),
            pltpu.SemaphoreType.DMA((32,)),
            pltpu.SemaphoreType.DMA((2, RING * RING + 1)),
            pltpu.SemaphoreType.DMA((40,)),
            pltpu.SemaphoreType.DMA((40,)),
        ],
        cost_estimate=pl.CostEstimate(flops=7_000_000_000, bytes_accessed=14_000_000, transcendentals=0),
        compiler_params=pltpu.CompilerParams(collective_id=1, has_side_effects=True, vmem_limit_bytes=56 << 20),
    )(y_own, g_ffn[None, :], *weights)


def gather_weights(w_gate, w_up, w_down, group_size):
    cols = w_down.shape[0]
    pad = -(-cols // 16) * 16
    wide = lambda w: jnp.pad(w, ((0, pad - cols), (0, 0)))
    own = jnp.concatenate([wide(w_gate.T), wide(w_up.T), wide(w_down)], axis=0)
    cut = pad + (pad // 2) // 16 * 16
    plane = RING * RING * CORES
    up = [(d, (d + plane) % group_size) for d in range(group_size)]
    down = [(d, (d - plane) % group_size) for d in range(group_size)]
    swap = [(d, d ^ 1) for d in range(group_size)]
    left = lax.ppermute(own, 'sp', up)
    right = lax.ppermute(own, 'sp', down)
    far0 = lax.ppermute(left[:cut], 'sp', up)
    far1 = lax.ppermute(right[cut:], 'sp', down)
    mine = [own, left, right, far0, far1]
    return mine + [lax.ppermute(w, 'sp', swap) for w in mine], pad


def solution(mesh):
    group_size = mesh.shape['sp']
    tok_spec = P(('dp', 'sp'), None)
    row_spec = P(('dp', 'sp'))
    full_spec = P()
    col_spec = P(None, 'sp')

    def device_fn(x_blk, seg_blk, pos_blk, w_dq, g_q, w_uq, w_dkv, g_kv, w_ukv, w_o, g_ffn, w_gate, w_up, w_down):
        blk_len = x_blk.shape[0]
        tok_total = blk_len * group_size
        weights, pad = gather_weights(w_gate, w_up, w_down, group_size)

        q_lin = jnp.dot(x_blk, w_dq, preferred_element_type=jnp.float32)
        c_q = rms_norm(q_lin, g_q).astype(jnp.bfloat16)
        kv_lin = jnp.dot(x_blk, w_dkv, preferred_element_type=jnp.float32)
        c_kv = rms_norm(kv_lin[:, :KV_LATENT], g_kv).astype(jnp.bfloat16)
        k_rope = apply_rope(kv_lin[:, KV_LATENT:], pos_blk).astype(jnp.bfloat16)
        pos_hi = (pos_blk // 64).astype(jnp.bfloat16)[:, None]
        pos_lo = (pos_blk % 64).astype(jnp.bfloat16)[:, None]
        spare = jnp.zeros((blk_len, NOPE_DIM - ROPE_DIM - 2), jnp.bfloat16)
        split = KV_LATENT
        q_rest = jnp.concatenate([c_q[:, split:], k_rope, pos_hi, pos_lo, spare], axis=1)
        blk = min(512, tok_total)
        qt, k, vt, pos_rows = gather_qkv(c_kv, c_q[:, :split], q_rest, w_uq, w_ukv, tok_total, blk)
        o_loc = attention(qt, k, vt, pos_rows[:1], blk)
        y_att = project(o_loc, w_o, group_size, 12)
        return ffn(y_att, g_ffn, weights, pad)

    return jax.shard_map(device_fn, mesh=mesh, in_specs=(tok_spec, row_spec, row_spec, full_spec, full_spec, col_spec, full_spec, full_spec, col_spec, full_spec, full_spec, col_spec, col_spec, P('sp', None)), out_specs=tok_spec, check_vma=False)
```

profile of v0, /device:TPU:0, one launch (start us, length us, event | category | flops | bytes accessed | tf_op | source)
XLA Modules:
  0.0 250.9 jit_solution(13379901091180089216)
XLA Ops:
  0.0 0.0 copy-start
  0.0 2.7 %fusion.5.rest_0_ = bf16[240,3584]{1,0:T(8,128)(2,1)} fusion(bf16[72,3584]{1,0:T(8,128)(2,1)} %param.26, bf16[72,3584]{1,0:T(8,128)(2,1)} %bitcast.35, bf16[72,3584]{1,0:T(8,128)(2,1)} %bitcast.36), kind=kLoop, calls=%fused_computation.9 | loop fusion | flops 12042240 | bytes 3268608 | tf_op jit(solution)/shard_map/concatenate | solution.py:667
  2.7 4.2 %collective-permute-start.1 = (bf16[240,3584]{1,0:T(8,128)(2,1)}, bf16[240,3584]{1,0:T(8,128)(2,1)}, u32[]{:S(2)}, u32[]{:S(2)}) collective-permute-start(bf16[240,3584]{1,0:T(8,128)(2,1)} %fusion.5.rest_0_), channel_id=1, source_target_pairs={{0,96},{1,97},{2,98},{3,99},{4,100},{5,101},{6,102},{7,103},{8,104... | collective-permute-start | bytes 5160968 | tf_op jit(solution)/shard_map/ppermute | solution.py:674
  6.9 0.0 collective-permute-start
  6.9 0.0 collective-permute-start.4
  6.9 0.0 copy-done
  6.9 3.7 %multiply_reduce_fusion = (f32[32]{0:T(128)S(1)}, f32[32,768]{1,0:T(8,128)S(1)}) fusion(bf16[32,3584]{1,0:T(8,128)(2,1)S(1)} %copy-done, bf16[3584,768]{1,0:T(8,128)(2,1)} %param.16), kind=kOutput, calls=%fused_computation.11 | convolution fusion | flops 176209888 | bytes 5832832 | tf_op jit(solution)/shard_map/dot_general | solution.py:693
  10.6 0.0 copy-start.11
  10.6 0.0 copy-start.10
  10.7 0.0 copy-done.9
  10.7 0.1 multiply_convert_fusion
  10.8 0.0 copy-done.7
  10.9 1.3 fusion.16
  12.1 0.0 copy-done.11
  12.2 0.1 copy.14
  12.3 0.1 copy.15
  12.4 1.0 constant_dynamic-slice_fusion.2
  13.4 0.1 copy.24
  13.5 0.1 multiply_reduce_fusion.1
  13.6 0.0 copy-done.10
  13.6 1.1 constant_dynamic-slice_fusion.1
  14.8 0.1 copy.20
  14.9 1.1 dynamic-slice.5
  16.0 0.1 copy.21
  16.1 0.1 fusion.13
  16.2 0.1 select_convert_fusion.pick
  16.3 0.1 concatenate.9.qb_own
  16.4 0.1 multiply_convert_fusion.1.kv_own
  16.5 66.0 %gather_qkv.1 = (bf16[256,4096]{1,0:T(8,128)(2,1)S(1)}, bf16[4096,256]{1,0:T(8,128)(2,1)S(1)}, bf16[128,4096]{1,0:T(8,128)(2,1)S(1)}, f32[8,4096]{1,0:T(8,128)S(1)}) custom-call(bf16[32,512]{1,0:T(8,128)(2,1)S(1)} %multiply_convert_fusion.1.kv_own, bf16[32,512]{1,0:T(8,128)(2,1)S(1)} %slice.60.qa_own, bf16[32,384]{1,0:T(8,128)(2,1)S(1)} %concatenate.9.qb_own, ...), custom_call_target="tpu_custom_call" | custom-call | flops 4000000000 | bytes 6000000 | tf_op jit(solution)/shard_map/gather_qkv/pallas_call | solution.py:232
  82.5 0.0 copy-start.3
  82.5 0.0 copy-start.5
  82.6 0.0 collective-permute-done.1.rest_2_
  82.6 2.9 %slice.65 = bf16[128,3584]{1,0:T(8,128)(2,1)} slice(bf16[240,3584]{1,0:T(8,128)(2,1)} %collective-permute-done.1.rest_2_), slice={[112:240], [0:3584]} | slice | bytes 1835008 | tf_op jit(solution)/shard_map/slice | solution.py:676
  85.5 4.7 %collective-permute-start.3 = (bf16[128,3584]{1,0:T(8,128)(2,1)}, bf16[128,3584]{1,0:T(8,128)(2,1)}, u32[]{:S(2)}, u32[]{:S(2)}) collective-permute-start(bf16[128,3584]{1,0:T(8,128)(2,1)} %slice.65), channel_id=1, source_target_pairs={{0,96},{1,97},{2,98},{3,99},{4,100},{5,101},{6,102},{7,103},{8,104... | collective-permute-start | bytes 2752520 | tf_op jit(solution)/shard_map/ppermute | solution.py:676
  90.1 0.0 collective-permute-done.rest_1_
  90.1 1.2 slice.64
  91.3 0.1 collective-permute-start.2
  91.4 0.4 collective-permute-start.5
  91.8 0.0 copy-done.3
  91.8 0.2 collective-permute-start.6
  92.0 0.0 copy-done.5
  92.0 0.1 slice.55
  92.1 0.1 slice.56
  92.3 20.5 %collective-permute-done.2.rest_3_ = bf16[112,3584]{1,0:T(8,128)(2,1)} collective-permute-done((bf16[112,3584]{1,0:T(8,128)(2,1)S(1)}, bf16[112,3584]{1,0:T(8,128)(2,1)}, u32[]{:S(2)}, u32[]{:S(2)}) %collective-permute-start.2) | collective-permute-done | bytes 802848 | tf_op jit(solution)/shard_map/ppermute | solution.py:675
  112.7 0.0 collective-permute-start.7
  112.7 0.0 collective-permute-done.3.rest_4_
  112.7 0.5 collective-permute-start.8
  113.2 1.6 copy-done.4
  114.8 1.2 copy-done.6
  116.0 23.4 %attention.1.o_ref = bf16[4096,128]{1,0:T(8,128)(2,1)S(1)} custom-call(s32[8]{0:T(128)S(1)} %get-tuple-element.14.lo_ref, s32[8]{0:T(128)S(1)} %get-tuple-element.13.clear_ref, bf16[256,4096]{1,0:T(8,128)(2,1)S(1)} %get-tuple-element.10.q_ref, bf16[4096,256]{1,0:T(8,128)(2,1)S(1)} %copy-done.4, bf16[128,4096]{1,0:T(8,128)(2,1)S(1)} %copy-done.6, ...), custom_call_target="tpu_custom_call" | custom-call | flops 10000000000 | bytes 8000000 | tf_op jit(solution)/shard_map/attention/pallas_call | solution.py:290
  139.4 0.0 copy-start.2
  139.4 1.0 copy-done.2
  140.4 0.0 copy-done.8
  140.4 0.6 broadcast_in_dim.63.g_ref
  141.0 32.3 %project.1.y_ref = bf16[32,3584]{1,0:T(8,128)(2,1)} custom-call(bf16[4096,128]{1,0:T(8,128)(2,1)} %copy-done.2, bf16[16384,3584]{1,0:T(8,128)(2,1)} %wo_ref.1), custom_call_target="tpu_custom_call" | custom-call | flops 4000000000 | bytes 60000000 | tf_op jit(solution)/shard_map/project/pallas_call | solution.py:419
  173.4 0.0 collective-permute-done.4.rest_5_
  173.4 0.0 collective-permute-done.7.rest_8_
  173.4 0.0 collective-permute-done.5.rest_6_
  173.4 0.0 collective-permute-done.6.rest_7_
  173.4 0.0 collective-permute-done.8.rest_9_
  173.4 0.8 copy-done.13
  174.3 1.0 copy-done.12
  175.2 74.0 %ffn.1 = bf16[32,3584]{1,0:T(8,128)(2,1)} custom-call(bf16[32,3584]{1,0:T(8,128)(2,1)} %project.1.y_ref, bf16[1,3584]{1,0:T(2,128)(2,1)} %broadcast_in_dim.63.g_ref, bf16[240,3584]{1,0:T(8,128)(2,1)} %fusion.5.rest_0_, bf16[240,3584]{1,0:T(8,128)(2,1)} %collective-permute-done.rest_1_, bf16[240,3584]{1,0:T(8,128)(2,1)} %collective-permute-done.1.rest_2_, ...), custom_call_target="tpu_custom_call" | custom-call | flops 7000000000 | bytes 14000000 | tf_op jit(solution)/shard_map/ffn/pallas_call | solution.py:631
  249.3 1.6 copy.26
  (24 shorter events, 0.2 us)
Async XLA Ops:
  0.0 6.9 %copy-start = (bf16[32,3584]{1,0:T(8,128)(2,1)S(1)}, bf16[32,3584]{1,0:T(8,128)(2,1)}, u32[]{:S(2)}) copy-start(bf16[32,3584]{1,0:T(8,128)(2,1)} %param.14) | copy-start | bytes 688132
  2.7 8.0 %copy-start.9 = (bf16[768]{0:T(1024)(128)(2,1)S(1)}, bf16[768]{0:T(1024)(128)(2,1)}, u32[]{:S(2)}) copy-start(bf16[768]{0:T(1024)(128)(2,1)} %param.17) | copy-start | bytes 4612
  2.7 8.1 %copy-start.7 = (bf16[3584,576]{0,1:T(8,128)(2,1)S(1)}, bf16[3584,576]{0,1:T(8,128)(2,1)}, u32[]{:S(2)}) copy-start(bf16[3584,576]{0,1:T(8,128)(2,1)} %param.19) | copy-start | bytes 12386308
  2.7 79.9 %collective-permute-start.1 = (bf16[240,3584]{1,0:T(8,128)(2,1)}, bf16[240,3584]{1,0:T(8,128)(2,1)}, u32[]{:S(2)}, u32[]{:S(2)}) collective-permute-start(bf16[240,3584]{1,0:T(8,128)(2,1)} %fusion.5.rest_0_), channel_id=1, source_target_pairs={{0,96},{1,97},{2,98},{3,99},{4,100},{5,101},{6,102},{7,103},{8,104... | collective-permute-start | bytes 5160968 | tf_op jit(solution)/shard_map/ppermute | solution.py:674
  6.9 83.3 %collective-permute-start = (bf16[240,3584]{1,0:T(8,128)(2,1)}, bf16[240,3584]{1,0:T(8,128)(2,1)}, u32[]{:S(2)}, u32[]{:S(2)}) collective-permute-start(bf16[240,3584]{1,0:T(8,128)(2,1)} %fusion.5.rest_0_), channel_id=1, source_target_pairs={{0,32},{1,33},{2,34},{3,35},{4,36},{5,37},{6,38},{7,39},{8,40},{9,... | collective-permute-start | bytes 5160968 | tf_op jit(solution)/shard_map/ppermute | solution.py:673
  6.9 166.5 %collective-permute-start.4 = (bf16[240,3584]{1,0:T(8,128)(2,1)}, bf16[240,3584]{1,0:T(8,128)(2,1)}, u32[]{:S(2)}, u32[]{:S(2)}) collective-permute-start(bf16[240,3584]{1,0:T(8,128)(2,1)} %fusion.5.rest_0_), channel_id=1, source_target_pairs={{0,1},{1,0},{2,3},{3,2},{4,5},{5,4},{6,7},{7,6},{8,9},{9,8},{10,11... | collective-permute-start | bytes 5160968 | tf_op jit(solution)/shard_map/ppermute | solution.py:678
  10.6 1.5 copy-start.11
  10.6 3.0 %copy-start.10 = (bf16[512]{0:T(512)(128)(2,1)S(1)}, bf16[512]{0:T(512)(128)(2,1)}, u32[]{:S(2)}) copy-start(bf16[512]{0:T(512)(128)(2,1)} %param.20) | copy-start | bytes 3076
  82.5 9.3 %copy-start.3 = (bf16[4096,256]{1,0:T(8,128)(2,1)}, bf16[4096,256]{1,0:T(8,128)(2,1)S(1)}, u32[]{:S(2)}) copy-start(bf16[4096,256]{1,0:T(8,128)(2,1)S(1)} %get-tuple-element.11.k_ref) | copy-start | bytes 6291460
  82.5 9.5 %copy-start.5 = (bf16[128,4096]{1,0:T(8,128)(2,1)}, bf16[128,4096]{1,0:T(8,128)(2,1)S(1)}, u32[]{:S(2)}) copy-start(bf16[128,4096]{1,0:T(8,128)(2,1)S(1)} %get-tuple-element.12.v_ref) | copy-start | bytes 3145732
  85.5 27.3 %collective-permute-start.3 = (bf16[128,3584]{1,0:T(8,128)(2,1)}, bf16[128,3584]{1,0:T(8,128)(2,1)}, u32[]{:S(2)}, u32[]{:S(2)}) collective-permute-start(bf16[128,3584]{1,0:T(8,128)(2,1)} %slice.65), channel_id=1, source_target_pairs={{0,96},{1,97},{2,98},{3,99},{4,100},{5,101},{6,102},{7,103},{8,104... | collective-permute-start | bytes 2752520 | tf_op jit(solution)/shard_map/ppermute | solution.py:676
  91.3 21.4 %collective-permute-start.2 = (bf16[112,3584]{1,0:T(8,128)(2,1)S(1)}, bf16[112,3584]{1,0:T(8,128)(2,1)}, u32[]{:S(2)}, u32[]{:S(2)}) collective-permute-start(bf16[112,3584]{1,0:T(8,128)(2,1)S(1)} %slice.64), channel_id=1, source_target_pairs={{0,32},{1,33},{2,34},{3,35},{4,36},{5,37},{6,38},{7,39},{8,40},{9,... | collective-permute-start | bytes 2408456 | tf_op jit(solution)/shard_map/ppermute | solution.py:675
  91.4 82.0 %collective-permute-start.5 = (bf16[240,3584]{1,0:T(8,128)(2,1)}, bf16[240,3584]{1,0:T(8,128)(2,1)}, u32[]{:S(2)}, u32[]{:S(2)}) collective-permute-start(bf16[240,3584]{1,0:T(8,128)(2,1)} %collective-permute-done.rest_1_), channel_id=1, source_target_pairs={{0,1},{1,0},{2,3},{3,2},{4,5},{5,4},{6,7},{7,6},{8,9},{9,8},{10,11... | collective-permute-start | bytes 5160968 | tf_op jit(solution)/shard_map/ppermute | solution.py:678
  91.8 81.6 %collective-permute-start.6 = (bf16[240,3584]{1,0:T(8,128)(2,1)}, bf16[240,3584]{1,0:T(8,128)(2,1)}, u32[]{:S(2)}, u32[]{:S(2)}) collective-permute-start(bf16[240,3584]{1,0:T(8,128)(2,1)} %collective-permute-done.1.rest_2_), channel_id=1, source_target_pairs={{0,1},{1,0},{2,3},{3,2},{4,5},{5,4},{6,7},{7,6},{8,9},{9,8},{10,11... | collective-permute-start | bytes 5160968 | tf_op jit(solution)/shard_map/ppermute | solution.py:678
  112.7 60.7 %collective-permute-start.7 = (bf16[112,3584]{1,0:T(8,128)(2,1)}, bf16[112,3584]{1,0:T(8,128)(2,1)S(1)}, u32[]{:S(2)}, u32[]{:S(2)}) collective-permute-start(bf16[112,3584]{1,0:T(8,128)(2,1)} %collective-permute-done.2.rest_3_), channel_id=1, source_target_pairs={{0,1},{1,0},{2,3},{3,2},{4,5},{5,4},{6,7},{7,6},{8,9},{9,8},{10,11... | collective-permute-start | bytes 2408456 | tf_op jit(solution)/shard_map/ppermute | solution.py:678
  112.7 60.7 %collective-permute-start.8 = (bf16[128,3584]{1,0:T(8,128)(2,1)}, bf16[128,3584]{1,0:T(8,128)(2,1)S(1)}, u32[]{:S(2)}, u32[]{:S(2)}) collective-permute-start(bf16[128,3584]{1,0:T(8,128)(2,1)} %collective-permute-done.3.rest_4_), channel_id=1, source_target_pairs={{0,1},{1,0},{2,3},{3,2},{4,5},{5,4},{6,7},{7,6},{8,9},{9,8},{10,11... | collective-permute-start | bytes 2752520 | tf_op jit(solution)/shard_map/ppermute | solution.py:678
  113.2 1.6 copy-start.4
  114.8 1.2 copy-start.6
  116.0 24.4 %copy-start.8 = (bf16[3584]{0:T(1024)(128)(2,1)S(1)}, bf16[3584]{0:T(1024)(128)(2,1)}, u32[]{:S(2)}) copy-start(bf16[3584]{0:T(1024)(128)(2,1)} %param.23) | copy-start | bytes 21508
  139.4 1.0 copy-start.2
  173.4 0.9 copy-start.13
  174.3 1.0 copy-start.12
  175.2 75.7 %copy-start.1 = (bf16[32,3584]{1,0:T(8,128)(2,1)S(1)}, bf16[32,3584]{1,0:T(8,128)(2,1)}, u32[]{:S(2)}) copy-start(bf16[32,3584]{1,0:T(8,128)(2,1)} %param.14) | copy-start | bytes 688132
where the time goes:
time: 253 us; the launch traced here: 251 us
  Pallas kernels  196 us (77%)
  waiting for transfers between devices  20.5 us (8%)
  local copies, waits for them, and re-layouts  16 us (6%)
  starting transfers between devices  10 us (4%)
  matrix products  4.97 us (2%)
  other arithmetic  3.32 us (1%)
    pallas_call x1, Pallas kernels, ffn(): pl.pallas_call(functools.partial(ffn_kernel, dim=dim, pad=pad, sub=sub, t...  74 us
    pallas_call x1, Pallas kernels, gather_qkv(): pl.pallas_call(functools.partial(qkv_kernel, blk=blk), name='gather_qkv',...  66 us
    pallas_call x1, Pallas kernels, project(): pl.pallas_call(functools.partial(project_kernel, n_buf=n_buf), name='proj...  32.3 us
    pallas_call x1, Pallas kernels, attention(): pl.pallas_call(functools.partial(attn_kernel, blk=blk), name='attention',...  23.4 us
    ppermute x1, waiting for transfers between devices, gather_weights(): far0 = lax.ppermute(left[:cut], 'sp', up)  20.5 us
    unnamed x32, local copies, waits for them, and re-layouts  7.65 us
  transfers between devices with their start and end apart: 9, of which 1 were waited for; matrix products, arithmetic and copies ran while one was open for 6% of the time, Pallas kernels for 49%

commit v1 on v0

--- a/solution.py
+++ b/solution.py
@@ -250,8 +250,10 @@
     )(kv_own, qa_own, qb_own, w_uq[:wa].T, w_uq[wa:].T, w_ukv[:, :NOPE_DIM], w_ukv[:, NOPE_DIM:].T, inv_freq[:, None], pick)
 
 
-def attn_kernel(lo_ref, clear_ref, q_ref, k_ref, v_ref, start_ref, pos_ref, o_ref, acc_ref, *, blk):
+def attn_kernel(q_ref, k_ref, v_ref, pos_ref, o_ref, acc_ref, *, blk):
     i = pl.program_id(0)
+    pos = pos_ref[0:1].astype(jnp.int32)
+    start = i * blk + lax.broadcasted_iota(jnp.int32, (1, blk), 1) - pos
     acc_ref[...] = jnp.zeros_like(acc_ref)
 
     def block(masked, kb, carry):
@@ -260,8 +262,8 @@
         s = jnp.dot(k_ref[rows, :], q_ref[...], preferred_element_type=jnp.float32)
         if masked:
             key = kb * blk + lax.broadcasted_iota(jnp.int32, s.shape, 0)
-            back = key - start_ref[...]
-            s = jnp.where((back >= 0) & (back <= pos_ref[...]), s, MASKED)
+            back = key - start
+            s = jnp.where((back >= 0) & (back <= pos), s, MASKED)
         m_new = jnp.maximum(m_old, jnp.max(s, axis=0, keepdims=True))
         p = jnp.exp2((s - m_new) * (SCORE_SCALE * LOG2E))
         alpha = jnp.exp2((m_old - m_new) * (SCORE_SCALE * LOG2E))
@@ -270,37 +272,30 @@
         return m_new, l_new
 
     carry = (jnp.full((1, blk), MASKED, jnp.float32), jnp.zeros((1, blk), jnp.float32))
-    lo = lo_ref[i]
-    clear = clear_ref[i]
+    lo = jnp.min(start) // blk
+    clear = jnp.minimum((jnp.max(start) + (blk - 1)) // blk, i)
     carry = lax.fori_loop(lo, clear, functools.partial(block, True), carry)
     carry = lax.fori_loop(clear, i, functools.partial(block, False), carry)
     _, total = block(True, i, carry)
     o_ref[...] = (acc_ref[...] / total).T.astype(jnp.bfloat16)
 
 
-def attention(qt, k, vt, pos_row, blk):
+def attention(qt, k, vt, pos_rows, blk):
     tok = k.shape[0]
     n_blk = tok // blk
-    pos_all = pos_row.astype(jnp.int32)
-    start = jnp.arange(tok, dtype=jnp.int32)[None, :] - pos_all
-    lo = start[0, ::blk] // blk
-    clear = jnp.clip((start[0, blk - 1::blk] + blk - 1) // blk, lo, jnp.arange(n_blk, dtype=jnp.int32))
-    whole = lambda a: pl.BlockSpec(a.shape, lambda i, *_: (0, 0), pipeline_mode=pl.Buffered(1))
-    lane_blk = lambda r: pl.BlockSpec((r, blk), lambda i, *_: (0, i))
+    whole = lambda a: pl.BlockSpec(a.shape, lambda i: (0, 0), pipeline_mode=pl.Buffered(1))
+    lane_blk = lambda a: pl.BlockSpec((a.shape[0], blk), lambda i: (0, i))
     return pl.pallas_call(
         functools.partial(attn_kernel, blk=blk),
         name="attention",
         out_shape=jax.ShapeDtypeStruct((tok, VALUE_DIM), jnp.bfloat16),
-        grid_spec=pltpu.PrefetchScalarGridSpec(
-            num_scalar_prefetch=2,
-            grid=(n_blk,),
-            in_specs=[lane_blk(2 * NOPE_DIM), whole(k), whole(vt), lane_blk(1), lane_blk(1)],
-            out_specs=pl.BlockSpec((blk, VALUE_DIM), lambda i, *_: (i, 0)),
-            scratch_shapes=[pltpu.VMEM((VALUE_DIM, blk), jnp.float32)],
-        ),
+        grid=(n_blk,),
+        in_specs=[lane_blk(qt), whole(k), whole(vt), lane_blk(pos_rows)],
+        out_specs=pl.BlockSpec((blk, VALUE_DIM), lambda i: (i, 0)),
+        scratch_shapes=[pltpu.VMEM((VALUE_DIM, blk), jnp.float32)],
         cost_estimate=pl.CostEstimate(flops=10_000_000_000, bytes_accessed=8_000_000, transcendentals=9_000_000),
         compiler_params=pltpu.CompilerParams(dimension_semantics=("arbitrary",), vmem_limit_bytes=40 << 20),
-    )(lo, clear, qt, k, vt, start, pos_all)
+    )(qt, k, vt, pos_rows)
 
 
 def project_kernel(o_ref, wo_ref, y_ref, o_all, w_buf, acc, y_half, y_in, w_sem, send_sem, recv_sem, fwd_send, fwd_recv,
@@ -441,25 +436,22 @@
 
 
 def ffn_kernel(y_ref, g_ref, *rest, dim, pad, sub, tile_n):
-    n_wt = 10
+    n_wt = 5
     weights = rest[:n_wt]
     (out_ref, ybuf, wgu, wdn, hbuf, gubuf, part, far_l, far_r, in_l, in_r, far2_l, far2_r, in2_l, in2_r,
-     w_sem, ag_send, ag_recv, rs_send, rs_recv) = rest[n_wt:]
-    me = lax.axis_index("sp")
-    core = lax.rem(me, CORES)
-    x = lax.rem(me // CORES, RING)
-    y = lax.rem(me // (CORES * RING), RING)
-    z = me // (CORES * RING * RING)
-
-    def device(yy, xx):
-        return {"sp": ((z * RING + yy) * RING + xx) * CORES + core}
-
-    x_up, x_dn = device(y, lax.rem(x + 1, RING)), device(y, lax.rem(x + RING - 1, RING))
-    y_up, y_dn = device(lax.rem(y + 1, RING), x), device(lax.rem(y + RING - 1, RING), x)
+     w_sem, wx_send, wx_recv, ag_send, ag_recv, rs_send, rs_recv) = rest[n_wt:]
+    coord = my_coord()
+
+    def device(axis, by):
+        c = {**coord, axis: lax.rem(coord[axis] + (by % RING), RING) if axis != "core" else 1 - coord[axis]}
+        return {"sp": ((c["z"] * RING + c["y"]) * RING + c["x"]) * CORES + c["core"]}
+
+    x_up, x_dn, y_up, y_dn = device("x", 1), device("x", -1), device("y", 1), device("y", -1)
+    z_up, z_dn, partner = device("z", 1), device("z", -1), device("core", 1)
     up1, dn1, up2, dn2 = (x_up, y_up), (x_dn, y_dn), (y_up, x_up), (y_dn, x_dn)
 
     barrier = pltpu.get_barrier_semaphore()
-    for nb in (x_up, x_dn, y_up, y_dn):
+    for nb in (x_up, x_dn, y_up, y_dn, z_up, z_dn, partner):
         pl.semaphore_signal(barrier, inc=1, device_id=nb, device_id_type=pl.DeviceIdType.MESH)
 
     w_copies = []
@@ -469,23 +461,32 @@
         cp.start()
         w_copies.append(cp)
 
-    cut = weights[3].shape[0]
-    for side in range(2):
-        own, left, right, f0, f1 = weights[5 * side:5 * side + 5]
-        for n, blk in enumerate((own, left, right)):
-            r = (4 * side + n) * pad
-            fetch(blk.at[0:pad], wgu.at[r:r + pad])
-            fetch(blk.at[pad:2 * pad], wgu.at[8 * pad + r:8 * pad + r + pad])
-            fetch(blk.at[2 * pad:], wdn.at[r:r + pad])
-        r = (4 * side + 3) * pad
-        fetch(f0.at[0:pad], wgu.at[r:r + pad])
-        fetch(f0.at[pad:cut], wgu.at[8 * pad + r:8 * pad + r + cut - pad])
-        fetch(f1.at[0:2 * pad - cut], wgu.at[8 * pad + r + cut - pad:8 * pad + r + pad])
-        fetch(f1.at[2 * pad - cut:], wdn.at[r:r + pad])
+    up0 = 8 * pad
+    own, left_a, left_b, right_a, right_b = weights
+    cut = left_a.shape[0]
+    fetch(own.at[0:pad], wgu.at[0:pad])
+    fetch(own.at[pad:2 * pad], wgu.at[up0:up0 + pad])
+    fetch(own.at[2 * pad:], wdn.at[0:pad])
+    for n, (part_a, part_b) in ((1, (left_a, left_b)), (2, (right_a, right_b))):
+        r = n * pad
+        fetch(part_a.at[0:pad], wgu.at[r:r + pad])
+        fetch(part_a.at[pad:cut], wgu.at[up0 + r:up0 + r + cut - pad])
+        fetch(part_b.at[0:2 * pad - cut], wgu.at[up0 + r + cut - pad:up0 + r + pad])
+        fetch(part_b.at[2 * pad - cut:], wdn.at[r:r + pad])
+
+    wx_copies = []
+
+    def exchange(buf, src, dst, rows, dev):
+        n = len(wx_copies)
+        cp = pltpu.make_async_remote_copy(
+            src_ref=buf.at[src:src + rows], dst_ref=buf.at[dst:dst + rows], send_sem=wx_send.at[n], recv_sem=wx_recv.at[n],
+            device_id=dev, device_id_type=pl.DeviceIdType.MESH)
+        cp.start()
+        wx_copies.append(cp)
 
     for h in range(2):
         ybuf[h, 0] = y_ref[h * sub:(h + 1) * sub, :]
-    pl.semaphore_wait(barrier, 4)
+    pl.semaphore_wait(barrier, 7)
 
     cols = (slice(0, dim // 2), slice(dim // 2, dim))
     ag_copies = {}
@@ -510,6 +511,16 @@
     for h in range(2):
         ag_send_to(h, 0, 3, up2[h])
         ag_send_to(h, 0, 1, dn2[h])
+    for cp in w_copies:
+        cp.wait()
+    split = cut - pad
+    exchange(wgu, pad, 3 * pad, pad, z_up)
+    exchange(wgu, up0 + pad, up0 + 3 * pad, split, z_up)
+    exchange(wgu, up0 + 2 * pad + split, up0 + 3 * pad + split, pad - split, z_dn)
+    exchange(wdn, 2 * pad, 3 * pad, pad, z_dn)
+    exchange(wgu, 0, 4 * pad, 3 * pad, partner)
+    exchange(wgu, up0, up0 + 4 * pad, 3 * pad, partner)
+    exchange(wdn, 0, 4 * pad, 3 * pad, partner)
     for h in range(2):
         ag_copies[(h, 3 * RING, None)].wait_recv()
         ag_send_to(h, 3 * RING, far * RING, up1[h], 0)
@@ -531,8 +542,13 @@
         for h in range(2):
             ag_copies[(h, d1 * RING + d2, None)].wait_recv()
 
-    for cp in w_copies:
-        cp.wait()
+    for n in range(4):
+        wx_copies[n].wait_recv()
+    exchange(wgu, 3 * pad, 7 * pad, pad, partner)
+    exchange(wgu, up0 + 3 * pad, up0 + 7 * pad, pad, partner)
+    exchange(wdn, 3 * pad, 7 * pad, pad, partner)
+    for n in range(4, 10):
+        wx_copies[n].wait_recv()
 
     rows = 2 * RING * sub
     nt = (((1,), (1,)), ((), ()))
@@ -616,7 +632,7 @@
         rs_copies[("jr", h)].wait_recv()
         total = part[h, 0] + in2_l[h] + in2_r[h]
         out_ref[h * sub:(h + 1) * sub, :] = (ybuf[h, 0].astype(jnp.float32) + total).astype(jnp.bfloat16)
-    for cp in list(ag_copies.values()) + list(rs_copies.values()):
+    for cp in wx_copies + list(ag_copies.values()) + list(rs_copies.values()):
         cp.wait_send()
 
 
@@ -632,7 +648,7 @@
         functools.partial(ffn_kernel, dim=dim, pad=pad, sub=sub, tile_n=256 if (16 * pad) % 256 == 0 else 16 * pad),
         name="ffn",
         out_shape=jax.ShapeDtypeStruct((rows, dim), bf16),
-        in_specs=[vm, vm] + [hbm] * 10,
+        in_specs=[vm, vm] + [hbm] * 5,
         out_specs=vm,
         scratch_shapes=[
             pltpu.VMEM((2, RING * RING, sub, dim), bf16),
@@ -649,7 +665,9 @@
             pltpu.VMEM((2, sub, half), f32),
             pltpu.VMEM((2, sub, dim), f32),
             pltpu.VMEM((2, sub, dim), f32),
-            pltpu.SemaphoreType.DMA((26,)),
+            pltpu.SemaphoreType.DMA((11,)),
+            pltpu.SemaphoreType.DMA((10,)),
+            pltpu.SemaphoreType.DMA((10,)),
             pltpu.SemaphoreType.DMA((32,)),
             pltpu.SemaphoreType.DMA((2, RING * RING + 1)),
             pltpu.SemaphoreType.DMA((40,)),
@@ -660,22 +678,18 @@
     )(y_own, g_ffn[None, :], *weights)
 
 
-def gather_weights(w_gate, w_up, w_down, group_size):
+def weight_block(w_gate, w_up, w_down):
     cols = w_down.shape[0]
     pad = -(-cols // 16) * 16
     wide = lambda w: jnp.pad(w, ((0, pad - cols), (0, 0)))
-    own = jnp.concatenate([wide(w_gate.T), wide(w_up.T), wide(w_down)], axis=0)
-    cut = pad + (pad // 2) // 16 * 16
+    return jnp.concatenate([wide(w_gate.T), wide(w_up.T), wide(w_down)], axis=0), pad
+
+
+def from_z_neighbours(block, group_size):
     plane = RING * RING * CORES
     up = [(d, (d + plane) % group_size) for d in range(group_size)]
     down = [(d, (d - plane) % group_size) for d in range(group_size)]
-    swap = [(d, d ^ 1) for d in range(group_size)]
-    left = lax.ppermute(own, 'sp', up)
-    right = lax.ppermute(own, 'sp', down)
-    far0 = lax.ppermute(left[:cut], 'sp', up)
-    far1 = lax.ppermute(right[cut:], 'sp', down)
-    mine = [own, left, right, far0, far1]
-    return mine + [lax.ppermute(w, 'sp', swap) for w in mine], pad
+    return lax.ppermute(block, 'sp', up), lax.ppermute(block, 'sp', down)
 
 
 def solution(mesh):
@@ -688,7 +702,9 @@
     def device_fn(x_blk, seg_blk, pos_blk, w_dq, g_q, w_uq, w_dkv, g_kv, w_ukv, w_o, g_ffn, w_gate, w_up, w_down):
         blk_len = x_blk.shape[0]
         tok_total = blk_len * group_size
-        weights, pad = gather_weights(w_gate, w_up, w_down, group_size)
+        w_own, pad = weight_block(w_gate, w_up, w_down)
+        cut = pad + (pad // 2) // 16 * 16
+        left_a, right_a = from_z_neighbours(w_own[:cut], group_size)
 
         q_lin = jnp.dot(x_blk, w_dq, preferred_element_type=jnp.float32)
         c_q = rms_norm(q_lin, g_q).astype(jnp.bfloat16)
@@ -702,8 +718,10 @@
         q_rest = jnp.concatenate([c_q[:, split:], k_rope, pos_hi, pos_lo, spare], axis=1)
         blk = min(512, tok_total)
         qt, k, vt, pos_rows = gather_qkv(c_kv, c_q[:, :split], q_rest, w_uq, w_ukv, tok_total, blk)
-        o_loc = attention(qt, k, vt, pos_rows[:1], blk)
+        w_late, pos_rows = lax.optimization_barrier((w_own[cut:], pos_rows))
+        left_b, right_b = from_z_neighbours(w_late, group_size)
+        o_loc = attention(qt, k, vt, pos_rows, blk)
         y_att = project(o_loc, w_o, group_size, 12)
-        return ffn(y_att, g_ffn, weights, pad)
+        return ffn(y_att, g_ffn, (w_own, left_a, left_b, right_a, right_b), pad)
 
     return jax.shard_map(device_fn, mesh=mesh, in_specs=(tok_spec, row_spec, row_spec, full_spec, full_spec, col_spec, full_spec, full_spec, col_spec, full_spec, full_spec, col_spec, col_spec, P('sp', None)), out_specs=tok_spec, check_vma=False)

time: 253 us -> 207 us (0.82)
  waiting for transfers between devices: 20.5 us -> 0.01 us
  Pallas kernels: 196 us -> 179 us
  local copies, waits for them, and re-layouts: 16 us -> 10.5 us
  starting transfers between devices: 10 us -> 6.6 us
    ppermute x9 -> x4, waiting for transfers between devices: 20.5 us -> 0.01 us  [from_z_neighbours(): return (lax.ppermute(block, 'sp', up), lax.ppermute(block, 'sp', down))]
    pallas_call x1, Pallas kernels: 66 us -> 45.8 us  [gather_qkv(): pl.pallas_call(functools.partial(qkv_kernel, blk=blk), name='gather_qkv',...]
    slice x4 -> x0, local copies, waits for them, and re-layouts: 4.25 us -> none  [the longest x1 2.86 us: gather_weights(): far1 = lax.ppermute(right[cut:], 'sp', down)]
    pallas_call x1, Pallas kernels: 74 us -> 78 us  [ffn(): pl.pallas_call(functools.partial(ffn_kernel, dim=dim, pad=pad, sub=sub, t...]
    ppermute x9 -> x4, starting transfers between devices: 10 us -> 6.6 us  [from_z_neighbours(): return (lax.ppermute(block, 'sp', up), lax.ppermute(block, 'sp', down))]
    unnamed x32 -> x34, local copies, waits for them, and re-layouts: 7.65 us -> 6.02 us
  transfers between devices with their start and end apart: 9 -> 4, of which waited for: 1 -> 0; matrix products, arithmetic and copies ran while one was open for 6% -> 1% of each run, Pallas kernels for 49% -> 27%
where the time goes in v1:
time: 207 us; the launch traced here: 204 us
  Pallas kernels  179 us (86%)
  local copies, waits for them, and re-layouts  10.5 us (5%)
  starting transfers between devices  6.6 us (3%)
  matrix products  5.4 us (3%)
    pallas_call x1, Pallas kernels, ffn(): pl.pallas_call(functools.partial(ffn_kernel, dim=dim, pad=pad, sub=sub, t...  78 us
    pallas_call x1, Pallas kernels, gather_qkv(): pl.pallas_call(functools.partial(qkv_kernel, blk=blk), name='gather_qkv',...  45.8 us
    pallas_call x1, Pallas kernels, project(): pl.pallas_call(functools.partial(project_kernel, n_buf=n_buf), name='proj...  30.8 us
    pallas_call x1, Pallas kernels, attention(): pl.pallas_call(functools.partial(attn_kernel, blk=blk), name='attention',...  24.4 us
    ppermute x4, starting transfers between devices, from_z_neighbours(): return (lax.ppermute(block, 'sp', up), lax.ppermute(block, 'sp', down))  6.6 us
    unnamed x34, local copies, waits for them, and re-layouts  6.02 us
  transfers between devices with their start and end apart: 4, of which 0 were waited for; matrix products, arithmetic and copies ran while one was open for 1% of the time, Pallas kernels for 27%

profile of v1, /device:TPU:0, one launch (start us, length us, event | category | flops | bytes accessed | tf_op | source)
XLA Modules:
  0.0 203.9 jit_solution(1861722126885860081)
XLA Ops:
  0.0 0.0 copy-start
  0.0 0.0 copy-start.9
  0.0 0.0 copy-start.3
  0.0 0.9 copy-done
  0.9 4.1 %multiply_reduce_fusion = (f32[32]{0:T(128)S(1)}, f32[32,768]{1,0:T(8,128)S(1)}) fusion(bf16[32,3584]{1,0:T(8,128)(2,1)S(1)} %copy-done, bf16[3584,768]{1,0:T(8,128)(2,1)} %param.16), kind=kOutput, calls=%fused_computation.4 | convolution fusion | flops 176209888 | bytes 5832832 | tf_op jit(solution)/shard_map/dot_general | solution.py:709
  5.1 0.0 copy-start.11
  5.1 0.0 copy-start.10
  5.1 0.0 copy-done.9
  5.1 0.1 multiply_convert_fusion
  5.2 0.0 copy-start.7
  5.2 0.0 copy-start.4
  5.3 0.0 copy-done.3
  5.3 0.0 copy-start.5
  5.3 1.3 fusion.10
  6.6 0.0 copy-done.11
  6.6 0.1 copy.14
  6.7 0.1 copy.15
  6.8 1.0 constant_dynamic-slice_fusion.2
  7.8 0.1 copy.24
  8.0 0.1 multiply_reduce_fusion.1
  8.1 0.0 copy-done.10
  8.1 1.1 constant_dynamic-slice_fusion.1
  9.3 0.1 copy.20
  9.4 1.1 dynamic-slice.5
  10.5 0.1 copy.21
  10.6 0.0 copy-done.7
  10.6 0.0 copy-done.4
  10.6 0.0 slice-start
  10.6 0.0 copy-done.5
  10.7 0.1 fusion.7
  10.8 0.1 multiply_convert_fusion.1.kv_own
  10.9 0.1 select_convert_fusion.pick
  11.0 0.1 pad_maximum_fusion.1
  11.1 0.2 slice-done
  11.3 0.1 concatenate.15.qb_own
  11.4 0.0 copy-start.6
  11.4 45.8 %gather_qkv.1 = (bf16[256,4096]{1,0:T(8,128)(2,1)S(1)}, bf16[4096,256]{1,0:T(8,128)(2,1)S(1)}, bf16[128,4096]{1,0:T(8,128)(2,1)S(1)}, f32[8,4096]{1,0:T(8,128)S(1)}) custom-call(bf16[32,512]{1,0:T(8,128)(2,1)S(1)} %multiply_convert_fusion.1.kv_own, bf16[32,512]{1,0:T(8,128)(2,1)S(1)} %slice.50.qa_own, bf16[32,384]{1,0:T(8,128)(2,1)S(1)} %concatenate.15.qb_own, ...), custom_call_target="tpu_custom_call" | custom-call | flops 4000000000 | bytes 6000000 | tf_op jit(solution)/shard_map/gather_qkv/pallas_call | solution.py:232
  57.2 0.1 collective-permute-start.1
  57.3 3.2 %collective-permute-start.3 = (bf16[128,3584]{1,0:T(8,128)(2,1)S(1)}, bf16[128,3584]{1,0:T(8,128)(2,1)S(1)}, u32[]{:S(2)}, u32[]{:S(2)}) collective-permute-start(bf16[128,3584]{1,0:T(8,128)(2,1)S(1)} %pad_maximum_fusion.1), channel_id=1, source_target_pairs={{0,96},{1,97},{2,98},{3,99},{4,100},{5,101},{6,102},{7,103},{8,104... | collective-permute-start | bytes 2752520 | tf_op jit(solution)/shard_map/ppermute | solution.py:692
  60.5 0.0 copy-done.6
  60.6 0.1 pad_maximum_fusion.2
  60.6 0.1 collective-permute-start
  60.7 3.2 %collective-permute-start.2 = (bf16[112,3584]{1,0:T(8,128)(2,1)S(1)}, bf16[112,3584]{1,0:T(8,128)(2,1)}, u32[]{:S(2)}, u32[]{:S(2)}) collective-permute-start(bf16[112,3584]{1,0:T(8,128)(2,1)S(1)} %pad_maximum_fusion.2), channel_id=1, source_target_pairs={{0,96},{1,97},{2,98},{3,99},{4,100},{5,101},{6,102},{7,103},{8,104... | collective-permute-start | bytes 2408456 | tf_op jit(solution)/shard_map/ppermute | solution.py:692
  63.9 0.0 copy-start.8
  63.9 24.4 %attention.1.o_ref = bf16[4096,128]{1,0:T(8,128)(2,1)S(1)} custom-call(bf16[256,4096]{1,0:T(8,128)(2,1)S(1)} %get-tuple-element.11.q_ref, bf16[4096,256]{1,0:T(8,128)(2,1)S(1)} %get-tuple-element.12.k_ref, bf16[128,4096]{1,0:T(8,128)(2,1)S(1)} %get-tuple-element.13.v_ref, f32[8,4096]{1,0:T(8,128)S(1)} %get-tuple-element.15.pos_ref), custom_call_target="tpu_custom_call" | custom-call | flops 10000000000 | bytes 8000000 | tf_op jit(solution)/shard_map/attention/pallas_call | solution.py:288
  88.4 0.0 copy-start.2
  88.4 1.0 copy-done.2
  89.4 0.0 copy-done.8
  89.4 0.6 broadcast_in_dim.62.g_ref
  90.0 30.8 %project.1.y_ref = bf16[32,3584]{1,0:T(8,128)(2,1)} custom-call(bf16[4096,128]{1,0:T(8,128)(2,1)} %copy-done.2, bf16[16384,3584]{1,0:T(8,128)(2,1)} %wo_ref.1), custom_call_target="tpu_custom_call" | custom-call | flops 4000000000 | bytes 60000000 | tf_op jit(solution)/shard_map/project/pallas_call | solution.py:414
  120.8 1.3 pad_maximum_fusion.rest_0_
  122.1 0.0 collective-permute-done.rest_1_
  122.1 0.0 copy-start.14
  122.1 0.0 collective-permute-done.2.rest_3_
  122.1 0.0 collective-permute-done.1.rest_2_
  122.1 0.0 copy-start.12
  122.2 0.0 collective-permute-done.3.rest_4_
  122.2 0.9 copy-done.14
  123.0 0.3 copy-done.12
  123.3 0.0 copy-start.13
  123.3 0.9 copy-done.13
  124.3 78.0 %ffn.1 = bf16[32,3584]{1,0:T(8,128)(2,1)} custom-call(bf16[32,3584]{1,0:T(8,128)(2,1)} %project.1.y_ref, bf16[1,3584]{1,0:T(2,128)(2,1)} %broadcast_in_dim.62.g_ref, bf16[240,3584]{1,0:T(8,128)(2,1)} %pad_maximum_fusion.rest_0_, bf16[112,3584]{1,0:T(8,128)(2,1)} %copy-done.14, bf16[128,3584]{1,0:T(8,128)(2,1)} %copy-done.12, ...), custom_call_target="tpu_custom_call" | custom-call | flops 7000000000 | bytes 14000000 | tf_op jit(solution)/shard_map/ffn/pallas_call | solution.py:647
  202.2 1.6 copy.26
  203.9 0.0 copy-done.1
  (15 shorter events, 0.2 us)
Async XLA Ops:
  0.0 0.9 copy-start
  0.0 5.1 %copy-start.9 = (bf16[768]{0:T(1024)(128)(2,1)S(1)}, bf16[768]{0:T(1024)(128)(2,1)}, u32[]{:S(2)}) copy-start(bf16[768]{0:T(1024)(128)(2,1)} %param.17) | copy-start | bytes 4612
  0.0 5.3 %copy-start.3 = (bf16[3584,576]{0,1:T(8,128)(2,1)S(1)}, bf16[3584,576]{0,1:T(8,128)(2,1)}, u32[]{:S(2)}) copy-start(bf16[3584,576]{0,1:T(8,128)(2,1)} %param.19) | copy-start | bytes 12386308
  5.1 1.5 copy-start.11
  5.1 3.0 %copy-start.10 = (bf16[512]{0:T(512)(128)(2,1)S(1)}, bf16[512]{0:T(512)(128)(2,1)}, u32[]{:S(2)}) copy-start(bf16[512]{0:T(512)(128)(2,1)} %param.20) | copy-start | bytes 3076
  5.2 5.3 %copy-start.7 = (bf16[32,768]{1,0:T(8,128)(2,1)}, bf16[32,768]{1,0:T(8,128)(2,1)S(1)}, u32[]{:S(2)}) copy-start(bf16[32,768]{1,0:T(8,128)(2,1)S(1)} %multiply_convert_fusion) | copy-start | bytes 147460
  5.2 5.3 %copy-start.4 = (bf16[3584,72]{0,1:T(8,128)(2,1)S(1)}, bf16[3584,72]{0,1:T(8,128)(2,1)}, u32[]{:S(2)}) copy-start(bf16[3584,72]{0,1:T(8,128)(2,1)} %param.25) | copy-start | bytes 1548292
  5.3 5.3 %copy-start.5 = (bf16[72,3584]{1,0:T(8,128)(2,1)S(1)}, bf16[72,3584]{1,0:T(8,128)(2,1)}, u32[]{:S(2)}) copy-start(bf16[72,3584]{1,0:T(8,128)(2,1)} %param.26) | copy-start | bytes 1548292
  10.6 0.7 slice-start
  11.4 49.1 %copy-start.6 = (bf16[3584,72]{0,1:T(8,128)(2,1)S(1)}, bf16[3584,72]{0,1:T(8,128)(2,1)}, u32[]{:S(2)}) copy-start(bf16[3584,72]{0,1:T(8,128)(2,1)} %param.24) | copy-start | bytes 1548292
  57.2 64.9 %collective-permute-start.1 = (bf16[128,3584]{1,0:T(8,128)(2,1)S(1)}, bf16[128,3584]{1,0:T(8,128)(2,1)S(1)}, u32[]{:S(2)}, u32[]{:S(2)}) collective-permute-start(bf16[128,3584]{1,0:T(8,128)(2,1)S(1)} %pad_maximum_fusion.1), channel_id=1, source_target_pairs={{0,32},{1,33},{2,34},{3,35},{4,36},{5,37},{6,38},{7,39},{8,40},{9,... | collective-permute-start | bytes 2752520 | tf_op jit(solution)/shard_map/ppermute | solution.py:692
  57.3 64.8 %collective-permute-start.3 = (bf16[128,3584]{1,0:T(8,128)(2,1)S(1)}, bf16[128,3584]{1,0:T(8,128)(2,1)S(1)}, u32[]{:S(2)}, u32[]{:S(2)}) collective-permute-start(bf16[128,3584]{1,0:T(8,128)(2,1)S(1)} %pad_maximum_fusion.1), channel_id=1, source_target_pairs={{0,96},{1,97},{2,98},{3,99},{4,100},{5,101},{6,102},{7,103},{8,104... | collective-permute-start | bytes 2752520 | tf_op jit(solution)/shard_map/ppermute | solution.py:692
  60.6 61.5 %collective-permute-start = (bf16[112,3584]{1,0:T(8,128)(2,1)S(1)}, bf16[112,3584]{1,0:T(8,128)(2,1)S(1)}, u32[]{:S(2)}, u32[]{:S(2)}) collective-permute-start(bf16[112,3584]{1,0:T(8,128)(2,1)S(1)} %pad_maximum_fusion.2), channel_id=1, source_target_pairs={{0,32},{1,33},{2,34},{3,35},{4,36},{5,37},{6,38},{7,39},{8,40},{9,... | collective-permute-start | bytes 2408456 | tf_op jit(solution)/shard_map/ppermute | solution.py:692
  60.7 61.4 %collective-permute-start.2 = (bf16[112,3584]{1,0:T(8,128)(2,1)S(1)}, bf16[112,3584]{1,0:T(8,128)(2,1)}, u32[]{:S(2)}, u32[]{:S(2)}) collective-permute-start(bf16[112,3584]{1,0:T(8,128)(2,1)S(1)} %pad_maximum_fusion.2), channel_id=1, source_target_pairs={{0,96},{1,97},{2,98},{3,99},{4,100},{5,101},{6,102},{7,103},{8,104... | collective-permute-start | bytes 2408456 | tf_op jit(solution)/shard_map/ppermute | solution.py:692
  63.9 25.4 %copy-start.8 = (bf16[3584]{0:T(1024)(128)(2,1)S(1)}, bf16[3584]{0:T(1024)(128)(2,1)}, u32[]{:S(2)}) copy-start(bf16[3584]{0:T(1024)(128)(2,1)} %param.23) | copy-start | bytes 21508
  88.4 1.0 copy-start.2
  122.1 0.9 copy-start.14
  122.1 1.2 copy-start.12
  123.3 0.9 copy-start.13
  124.3 79.6 %copy-start.1 = (bf16[32,3584]{1,0:T(8,128)(2,1)S(1)}, bf16[32,3584]{1,0:T(8,128)(2,1)}, u32[]{:S(2)}) copy-start(bf16[32,3584]{1,0:T(8,128)(2,1)} %param.14) | copy-start | bytes 688132

commit v2 on v1

--- a/solution.py
+++ b/solution.py
@@ -250,140 +250,179 @@
     )(kv_own, qa_own, qb_own, w_uq[:wa].T, w_uq[wa:].T, w_ukv[:, :NOPE_DIM], w_ukv[:, NOPE_DIM:].T, inv_freq[:, None], pick)
 
 
-def attn_kernel(q_ref, k_ref, v_ref, pos_ref, o_ref, acc_ref, *, blk):
-    i = pl.program_id(0)
-    pos = pos_ref[0:1].astype(jnp.int32)
-    start = i * blk + lax.broadcasted_iota(jnp.int32, (1, blk), 1) - pos
-    acc_ref[...] = jnp.zeros_like(acc_ref)
-
-    def block(masked, kb, carry):
-        m_old, l_old = carry
-        rows = pl.ds(pl.multiple_of(kb * blk, blk), blk)
-        s = jnp.dot(k_ref[rows, :], q_ref[...], preferred_element_type=jnp.float32)
-        if masked:
-            key = kb * blk + lax.broadcasted_iota(jnp.int32, s.shape, 0)
-            back = key - start
-            s = jnp.where((back >= 0) & (back <= pos), s, MASKED)
-        m_new = jnp.maximum(m_old, jnp.max(s, axis=0, keepdims=True))
-        p = jnp.exp2((s - m_new) * (SCORE_SCALE * LOG2E))
-        alpha = jnp.exp2((m_old - m_new) * (SCORE_SCALE * LOG2E))
-        l_new = l_old * alpha + jnp.sum(p, axis=0, keepdims=True)
-        acc_ref[...] = acc_ref[...] * alpha + jnp.dot(v_ref[:, rows], p.astype(jnp.bfloat16), preferred_element_type=jnp.float32)
-        return m_new, l_new
-
-    carry = (jnp.full((1, blk), MASKED, jnp.float32), jnp.zeros((1, blk), jnp.float32))
-    lo = jnp.min(start) // blk
-    clear = jnp.minimum((jnp.max(start) + (blk - 1)) // blk, i)
-    carry = lax.fori_loop(lo, clear, functools.partial(block, True), carry)
-    carry = lax.fori_loop(clear, i, functools.partial(block, False), carry)
-    _, total = block(True, i, carry)
-    o_ref[...] = (acc_ref[...] / total).T.astype(jnp.bfloat16)
-
-
-def attention(qt, k, vt, pos_rows, blk):
-    tok = k.shape[0]
-    n_blk = tok // blk
-    whole = lambda a: pl.BlockSpec(a.shape, lambda i: (0, 0), pipeline_mode=pl.Buffered(1))
-    lane_blk = lambda a: pl.BlockSpec((a.shape[0], blk), lambda i: (0, i))
-    return pl.pallas_call(
-        functools.partial(attn_kernel, blk=blk),
-        name="attention",
-        out_shape=jax.ShapeDtypeStruct((tok, VALUE_DIM), jnp.bfloat16),
-        grid=(n_blk,),
-        in_specs=[lane_blk(qt), whole(k), whole(vt), lane_blk(pos_rows)],
-        out_specs=pl.BlockSpec((blk, VALUE_DIM), lambda i: (i, 0)),
-        scratch_shapes=[pltpu.VMEM((VALUE_DIM, blk), jnp.float32)],
-        cost_estimate=pl.CostEstimate(flops=10_000_000_000, bytes_accessed=8_000_000, transcendentals=9_000_000),
-        compiler_params=pltpu.CompilerParams(dimension_semantics=("arbitrary",), vmem_limit_bytes=40 << 20),
-    )(qt, k, vt, pos_rows)
-
-
-def project_kernel(o_ref, wo_ref, y_ref, o_all, w_buf, acc, y_half, y_in, w_sem, send_sem, recv_sem, fwd_send, fwd_recv,
-                   y_sem, *, n_buf):
+SUB_KEYS = 32
+
+
+def attend_kernel(q_ref, k_ref, v_ref, pos_ref, wo_ref, y_ref, s_even, s_odd, p_even, p_odd, acc_o, stats, o_buf, o_all, w_buf, acc, y_half, y_in,
+                  w_sem, send_sem, recv_sem, fwd_send, fwd_recv, y_sem, *, blk, n_buf):
     coord = my_coord()
     core, x, y, z = (coord[a] for a in ("core", "x", "y", "z"))
+    y_top, y_low = y // 2, lax.rem(y, 2)
     lines = RING * RING
-    chip_rows, head = o_all.shape[3], o_all.shape[4]
+    n_chips = lines * RING
+    chip_rows = o_all.shape[3]
     w_rows, cols = w_buf.shape[1], w_buf.shape[2]
     mesh_id = pl.DeviceIdType.MESH
-
-    def line_of(k):
-        return lax.rem(z + k // RING, RING) * RING + lax.rem(y + lax.rem(k, RING), RING)
-
-    def w_copy(k):
-        rows = pl.ds(pl.multiple_of(line_of(k) * w_rows, w_rows), w_rows)
+    n_blk = q_ref.shape[1] // blk
+    n_pairs = n_blk * (n_blk + 1) // 2
+    per_z = n_blk // RING
+    f32, bf16, i32 = jnp.float32, jnp.bfloat16, jnp.int32
+    scale = SCORE_SCALE * LOG2E
+
+    def line_of(n):
+        step = n // 2
+        return lax.rem(z + step // 2, RING) * RING + lax.rem(y_top + lax.rem(step, 2), 2) * 2 + lax.rem(y_low + lax.rem(n, 2), 2)
+
+    def block_of(n):
+        return lax.rem(z + RING - n // per_z, RING) * per_z + lax.rem(y_top + lax.rem(n, per_z), per_z)
+
+    def w_copy(n):
+        rows = pl.ds(pl.multiple_of(line_of(n) * w_rows, w_rows), w_rows)
         side = pl.ds(pl.multiple_of(core * cols, 128), cols)
-        slot = lax.rem(k, n_buf)
+        slot = lax.rem(n, n_buf)
         return pltpu.make_async_copy(wo_ref.at[rows, side], w_buf.at[slot], w_sem.at[slot])
 
     @pl.loop(0, n_buf)
-    def _(k):
-        w_copy(k).start()
-
-    def chip(k, dx):
-        zz = lax.rem(z + RING - k // RING, RING)
-        yy = lax.rem(y + RING - lax.rem(k, RING), RING)
-        xx = lax.rem(x + RING - dx, RING)
-        return (zz * RING + yy) * RING + xx
+    def _(n):
+        w_copy(n).start()
 
     me_chip = (z * RING + y) * RING + x
+    my_line = z * RING + y
     partner = {"sp": me_chip * CORES + 1 - core}
-    n_chips = lines * RING
 
     barrier = pltpu.get_barrier_semaphore()
     pl.semaphore_signal(barrier, inc=1, device_id=partner, device_id_type=mesh_id)
 
     @pl.loop(1, n_chips)
     def _(n):
-        to = {"sp": chip(n // RING, lax.rem(n, RING)) * CORES + core}
+        to = {"sp": lax.rem(me_chip + n, n_chips) * CORES + core}
         pl.semaphore_signal(barrier, inc=1, device_id=to, device_id_type=mesh_id)
 
-    my_line = z * RING + y
-    o_all[my_line, x, core] = o_ref[pl.ds(pl.multiple_of(me_chip * chip_rows, chip_rows), chip_rows), :]
+    for ref in (s_even, s_odd, p_even, p_odd):
+        ref[...] = jnp.zeros_like(ref)
+    acc_o[...] = jnp.zeros_like(acc_o)
+    stats[...] = jnp.zeros_like(stats)
+    acc[...] = jnp.zeros_like(acc)
     pl.semaphore_wait(barrier, n_chips)
 
-    def head_copy(n):
-        to = chip(n // RING, lax.rem(n, RING))
-        rows = pl.ds(pl.multiple_of(to * chip_rows, chip_rows), chip_rows)
+    chips_per_blk = blk // chip_rows
+
+    def send_block(i):
+        line0 = i * (chips_per_blk // RING)
+
+        @pl.loop(0, chips_per_blk)
+        def _(n):
+            yy = line0 + lax.rem(y_low + n // RING, chips_per_blk // RING)
+            to = yy * RING + lax.rem(x + lax.rem(n, RING), RING)
+            rows = pl.ds(pl.multiple_of(to * chip_rows, chip_rows), chip_rows)
+
+            @pl.when(to == me_chip)
+            def _():
+                o_all[my_line, x, core] = o_buf[rows, :]
+
+            @pl.when(to != me_chip)
+            def _():
+                pltpu.make_async_remote_copy(
+                    src_ref=o_buf.at[rows, :], dst_ref=o_all.at[my_line, x, core], send_sem=send_sem,
+                    recv_sem=recv_sem.at[my_line], device_id={"sp": to * CORES + core}, device_id_type=mesh_id).start()
+
+    sub = SUB_KEYS
+    fold = lambda v: v.reshape(sub // 8, 8, blk)
+    row_id = lax.broadcasted_iota(i32, (sub, blk), 0)
+
+    def body(t, s_a, s_b, p_a, p_b, carry):
+        (n_a, i_a, j_a), (i_b, j_b), (i_c, j_c), i_done = carry
+        m_old, l_old, top, alpha_c = stats[0:1], stats[1:2], stats[2:3], stats[3:4]
+
+        keys_c = pl.ds(pl.multiple_of(j_c * blk, blk), blk)
+        pv = jnp.dot(v_ref[:, keys_c], p_a[...], preferred_element_type=f32)
+        acc_o[...] = acc_o[...] * alpha_c + pv
+
+        first = j_b == 0
+        m_prev = jnp.where(first, MASKED, m_old)
+        m_new = jnp.maximum(m_prev, top)
+        alpha_b = jnp.where(first, 0.0, jnp.exp2((m_prev - m_new) * scale))
+        part = jnp.zeros((8, blk), f32)
+        for g in range(blk // sub):
+            p = jnp.exp2((s_b[g * sub:(g + 1) * sub, :] - m_new) * scale)
+            part = part + jnp.sum(fold(p), axis=0)
+            p_b[g * sub:(g + 1) * sub, :] = p.astype(bf16)
+        l_new = l_old * alpha_b + jnp.sum(part, axis=0, keepdims=True)
+
+        cols_a = pl.ds(pl.multiple_of(i_a * blk, blk), blk)
+        pos = pos_ref[0:1, cols_a].astype(i32)
+        first_key = i_a * blk + lax.broadcasted_iota(i32, (1, blk), 1) - pos - j_a * blk
+        reach = pos.astype(jnp.uint32)
+        peak = jnp.full((8, blk), MASKED, f32)
+        wide = blk // 2
+        for h in range(2):
+            keys_a = pl.ds(pl.multiple_of(j_a * blk + h * wide, wide), wide)
+            s = jnp.dot(k_ref[keys_a, :], q_ref[:, cols_a], preferred_element_type=f32)
+            for g in range(wide // sub):
+                back = row_id - (first_key - (h * wide + g * sub))
+                kept = jnp.where(back.astype(jnp.uint32) <= reach, s[g * sub:(g + 1) * sub], MASKED)
+                peak = jnp.maximum(peak, jnp.max(fold(kept), axis=0))
+                s_a[h * wide + g * sub:h * wide + (g + 1) * sub, :] = kept
+        top_new = jnp.max(peak, axis=0, keepdims=True)
+
+        @pl.when(i_done >= 0)
+        def _():
+            send_block(i_done)
+
+        done = (t >= 2) & (t < n_pairs + 2) & (j_c == i_c)
+
+        @pl.when(done)
+        def _():
+            o_buf[pl.ds(pl.multiple_of(i_c * blk, blk), blk), :] = (acc_o[...] / stats[1:2]).T.astype(bf16)
+
+        stats[0:1] = m_new
+        stats[1:2] = l_new
+        stats[2:3] = top_new
+        stats[3:4] = alpha_b
+
+        last = j_a == i_a
+        n_next = jnp.where(last, jnp.minimum(n_a + 1, n_blk - 1), n_a)
+        i_next = block_of(n_next)
+        j_next = jnp.where(last, 0, j_a + 1)
+        return (n_next, i_next, j_next), (i_a, j_a), (i_b, j_b), jnp.where(done, i_c, -1)
+
+    zero = jnp.int32(0)
+    def two(u, carry):
+        carry = body(2 * u, s_even, s_odd, p_even, p_odd, carry)
+        return body(2 * u + 1, s_odd, s_even, p_odd, p_even, carry)
+
+    lax.fori_loop(0, (n_pairs + 4) // 2, two, ((zero, block_of(zero), zero), (zero, zero), (zero, zero), jnp.int32(-1)))
+
+    def forward(n):
+        at = o_all.at[line_of(n), :, core]
         return pltpu.make_async_remote_copy(
-            src_ref=o_ref.at[rows, :], dst_ref=o_all.at[my_line, x, core], send_sem=send_sem, recv_sem=recv_sem.at[n // RING],
-            device_id={"sp": to * CORES + core}, device_id_type=mesh_id)
-
-    @pl.loop(1, n_chips)
+            src_ref=at, dst_ref=at, send_sem=fwd_send.at[n], recv_sem=fwd_recv.at[n], device_id=partner, device_id_type=mesh_id)
+
+    def arrive(n, n_heads):
+        at = o_all.at[line_of(n), pl.ds(0, n_heads), core]
+        pltpu.make_async_copy(at, at, recv_sem.at[line_of(n)]).wait()
+        forward(n).start()
+
+    arrive(0, RING - 1)
+
+    @pl.loop(0, lines)
     def _(n):
-        head_copy(n).start()
-
-    def forward(k):
-        at = o_all.at[line_of(k), :, core]
-        return pltpu.make_async_remote_copy(
-            src_ref=at, dst_ref=at, send_sem=fwd_send.at[k], recv_sem=fwd_recv.at[k], device_id=partner, device_id_type=mesh_id)
-
-    def arrive(k, n_heads):
-        at = o_all.at[line_of(k), pl.ds(0, n_heads), core]
-        pltpu.make_async_copy(at, at, recv_sem.at[k]).wait()
-        forward(k).start()
-
-    acc[...] = jnp.zeros_like(acc)
-    arrive(0, RING - 1)
-
-    @pl.loop(0, lines)
-    def _(k):
-        @pl.when(k + 1 < lines)
+        @pl.when(n + 1 < lines)
         def _():
-            arrive(k + 1, RING)
-
-        forward(k).wait_recv()
-        w_copy(k).wait()
-        line = line_of(k)
+            arrive(n + 1, RING)
+
+        forward(n).wait_recv()
+        w_copy(n).wait()
+        line = line_of(n)
         lhs = jnp.concatenate([o_all[line, i, j] for i in range(RING) for j in range(CORES)], axis=1)
-        acc[...] += jnp.dot(lhs, w_buf[lax.rem(k, n_buf)], preferred_element_type=jnp.float32)
-
-        @pl.when(k + n_buf < lines)
+        acc[...] += jnp.dot(lhs, w_buf[lax.rem(n, n_buf)], preferred_element_type=f32)
+
+        @pl.when(n + n_buf < lines)
         def _():
-            w_copy(k + n_buf).start()
+            w_copy(n + n_buf).start()
 
     own_rows = chip_rows // CORES
-    y_half[...] = acc[...].astype(jnp.bfloat16)
+    y_half[...] = acc[...].astype(bf16)
     swap = pltpu.make_async_remote_copy(
         src_ref=y_half.at[pl.ds(pl.multiple_of((1 - core) * own_rows, own_rows), own_rows), :], dst_ref=y_in,
         send_sem=y_sem.at[0], recv_sem=y_sem.at[1], device_id=partner, device_id_type=mesh_id)
@@ -396,33 +435,41 @@
     swap.wait_send()
 
     @pl.loop(0, lines)
-    def _(k):
-        forward(k).wait_send()
-
-    everything = o_ref.at[pl.ds(0, (n_chips - 1) * chip_rows), :]
+    def _(n):
+        forward(n).wait_send()
+
+    everything = o_buf.at[pl.ds(0, (n_chips - 1) * chip_rows), :]
     pltpu.make_async_copy(everything, everything, send_sem).wait()
 
 
-def project(o_loc, w_o, group_size, n_buf):
-    tok, head = o_loc.shape
+def attend_project(qt, k, vt, pos_rows, w_o, blk, group_size, n_buf):
+    tok = k.shape[0]
     own_rows = tok // group_size
     dim = w_o.shape[1]
     lines = RING * RING
     w_rows = w_o.shape[0] // lines
+    half = dim // CORES
     f32, bf16 = jnp.float32, jnp.bfloat16
     vm = pl.BlockSpec(memory_space=pltpu.VMEM)
     return pl.pallas_call(
-        functools.partial(project_kernel, n_buf=n_buf),
-        name="project",
+        functools.partial(attend_kernel, blk=blk, n_buf=n_buf),
+        name="attend_project",
         out_shape=jax.ShapeDtypeStruct((own_rows, dim), bf16),
-        in_specs=[vm, pl.BlockSpec(memory_space=pl.ANY)],
+        in_specs=[vm, vm, vm, vm, pl.BlockSpec(memory_space=pl.ANY)],
         out_specs=vm,
         scratch_shapes=[
-            pltpu.VMEM((lines, RING, CORES, CORES * own_rows, head), bf16),
-            pltpu.VMEM((n_buf, w_rows, dim // CORES), bf16),
-            pltpu.VMEM((CORES * own_rows, dim // CORES), f32),
-            pltpu.VMEM((CORES * own_rows, dim // CORES), bf16),
-            pltpu.VMEM((own_rows, dim // CORES), bf16),
+            pltpu.VMEM((blk, blk), f32),
+            pltpu.VMEM((blk, blk), f32),
+            pltpu.VMEM((blk, blk), bf16),
+            pltpu.VMEM((blk, blk), bf16),
+            pltpu.VMEM((VALUE_DIM, blk), f32),
+            pltpu.VMEM((8, blk), f32),
+            pltpu.VMEM((tok, VALUE_DIM), bf16),
+            pltpu.VMEM((lines, RING, CORES, CORES * own_rows, VALUE_DIM), bf16),
+            pltpu.VMEM((n_buf, w_rows, half), bf16),
+            pltpu.VMEM((CORES * own_rows, half), f32),
+            pltpu.VMEM((CORES * own_rows, half), bf16),
+            pltpu.VMEM((own_rows, half), bf16),
             pltpu.SemaphoreType.DMA((n_buf,)),
             pltpu.SemaphoreType.DMA,
             pltpu.SemaphoreType.DMA((lines,)),
@@ -430,9 +477,9 @@
             pltpu.SemaphoreType.DMA((lines,)),
             pltpu.SemaphoreType.DMA((2,)),
         ],
-        cost_estimate=pl.CostEstimate(flops=4_000_000_000, bytes_accessed=60_000_000, transcendentals=0),
-        compiler_params=pltpu.CompilerParams(collective_id=3, has_side_effects=True, vmem_limit_bytes=56 << 20),
-    )(o_loc, w_o)
+        cost_estimate=pl.CostEstimate(flops=14_000_000_000, bytes_accessed=70_000_000, transcendentals=9_000_000),
+        compiler_params=pltpu.CompilerParams(collective_id=3, has_side_effects=True, vmem_limit_bytes=58 << 20),
+    )(qt, k, vt, pos_rows, w_o)
 
 
 def ffn_kernel(y_ref, g_ref, *rest, dim, pad, sub, tile_n):
@@ -720,8 +767,7 @@
         qt, k, vt, pos_rows = gather_qkv(c_kv, c_q[:, :split], q_rest, w_uq, w_ukv, tok_total, blk)
         w_late, pos_rows = lax.optimization_barrier((w_own[cut:], pos_rows))
         left_b, right_b = from_z_neighbours(w_late, group_size)
-        o_loc = attention(qt, k, vt, pos_rows, blk)
-        y_att = project(o_loc, w_o, group_size, 12)
+        y_att = attend_project(qt, k, vt, pos_rows, w_o, blk, group_size, 11)
         return ffn(y_att, g_ffn, (w_own, left_a, left_b, right_a, right_b), pad)
 
     return jax.shard_map(device_fn, mesh=mesh, in_specs=(tok_spec, row_spec, row_spec, full_spec, full_spec, col_spec, full_spec, full_spec, col_spec, full_spec, full_spec, col_spec, col_spec, P('sp', None)), out_specs=tok_spec, check_vma=False)

time: 207 us -> 208 us (level)
  local copies, waits for them, and re-layouts: 10.5 us -> 12.8 us
    unnamed x34 -> x38, local copies, waits for them, and re-layouts: 6.02 us -> 8.36 us
    pallas_call x2 -> x1, Pallas kernels: 55.2 us -> 54.6 us  [attend_project(): pl.pallas_call(functools.partial(attend_kernel, blk=blk, n_buf=n_buf), na...]
  transfers between devices with their start and end apart: 4 -> 4, of which waited for: 0 -> 0; matrix products, arithmetic and copies ran while one was open for 1% -> 1% of each run, Pallas kernels for 27% -> 26%
where the time goes in v2:
time: 208 us; the launch traced here: 206 us
  Pallas kernels  179 us (86%)
  local copies, waits for them, and re-layouts  12.8 us (6%)
  starting transfers between devices  6.54 us (3%)
  matrix products  5.4 us (3%)
    pallas_call x1, Pallas kernels, ffn(): pl.pallas_call(functools.partial(ffn_kernel, dim=dim, pad=pad, sub=sub, t...  78.8 us
    pallas_call x1, Pallas kernels, attend_project(): pl.pallas_call(functools.partial(attend_kernel, blk=blk, n_buf=n_buf), na...  54.6 us
    pallas_call x1, Pallas kernels, gather_qkv(): pl.pallas_call(functools.partial(qkv_kernel, blk=blk), name='gather_qkv',...  45.8 us
    unnamed x38, local copies, waits for them, and re-layouts  8.36 us
    ppermute x4, starting transfers between devices, from_z_neighbours(): return (lax.ppermute(block, 'sp', up), lax.ppermute(block, 'sp', down))  6.54 us
  transfers between devices with their start and end apart: 4, of which 0 were waited for; matrix products, arithmetic and copies ran while one was open for 1% of the time, Pallas kernels for 26%

profile of v2, /device:TPU:0, one launch (start us, length us, event | category | flops | bytes accessed | tf_op | source)
XLA Modules:
  0.0 206.5 jit_solution(15876264751690728735)
XLA Ops:
  0.0 0.0 copy-start
  0.0 0.0 copy-start.12
  0.0 0.0 copy-start.6
  0.0 0.9 copy-done
  0.9 4.1 %multiply_reduce_fusion = (f32[32]{0:T(128)S(1)}, f32[32,768]{1,0:T(8,128)S(1)}) fusion(bf16[32,3584]{1,0:T(8,128)(2,1)S(1)} %copy-done, bf16[3584,768]{1,0:T(8,128)(2,1)} %param.16), kind=kOutput, calls=%fused_computation.4 | convolution fusion | flops 176209888 | bytes 5832832 | tf_op jit(solution)/shard_map/dot_general | solution.py:756
  5.1 0.0 copy-start.14
  5.1 0.0 copy-start.13
  5.1 0.0 copy-done.12
  5.1 0.1 multiply_convert_fusion
  5.2 0.0 copy-start.10
  5.2 0.0 copy-start.7
  5.3 0.0 copy-done.6
  5.3 0.0 copy-start.8
  5.3 1.3 fusion.10
  6.6 0.0 copy-done.14
  6.6 0.1 copy.14
  6.7 0.1 copy.15
  6.8 1.0 constant_dynamic-slice_fusion.2
  7.8 0.1 copy.24
  8.0 0.1 multiply_reduce_fusion.1
  8.1 0.0 copy-done.13
  8.1 1.1 constant_dynamic-slice_fusion.1
  9.3 0.1 copy.20
  9.4 1.1 dynamic-slice.5
  10.5 0.1 copy.21
  10.6 0.0 copy-done.10
  10.6 0.0 copy-done.7
  10.6 0.0 slice-start
  10.6 0.0 copy-done.8
  10.7 0.1 fusion.7
  10.8 0.1 multiply_convert_fusion.1.kv_own
  10.9 0.1 select_convert_fusion.pick
  11.0 0.1 pad_maximum_fusion.1
  11.1 0.2 slice-done
  11.3 0.1 concatenate.15.qb_own
  11.4 0.0 copy-start.9
  11.4 45.8 %gather_qkv.1 = (bf16[256,4096]{1,0:T(8,128)(2,1)S(1)}, bf16[4096,256]{1,0:T(8,128)(2,1)S(1)}, bf16[128,4096]{1,0:T(8,128)(2,1)S(1)}, f32[8,4096]{1,0:T(8,128)S(1)}) custom-call(bf16[32,512]{1,0:T(8,128)(2,1)S(1)} %multiply_convert_fusion.1.kv_own, bf16[32,512]{1,0:T(8,128)(2,1)S(1)} %slice.50.qa_own, bf16[32,384]{1,0:T(8,128)(2,1)S(1)} %concatenate.15.qb_own, ...), custom_call_target="tpu_custom_call" | custom-call | flops 4000000000 | bytes 6000000 | tf_op jit(solution)/shard_map/gather_qkv/pallas_call | solution.py:232
  57.2 0.0 copy-start.2
  57.2 1.3 copy-done.2
  58.6 0.0 copy-start.3
  58.6 1.3 copy-done.3
  59.9 0.0 copy-start.4
  59.9 1.0 copy-done.4
  60.8 0.7 copy-done.5
  61.5 0.0 collective-permute-start.1
  61.5 3.2 %collective-permute-start.3 = (bf16[128,3584]{1,0:T(8,128)(2,1)S(1)}, bf16[128,3584]{1,0:T(8,128)(2,1)}, u32[]{:S(2)}, u32[]{:S(2)}) collective-permute-start(bf16[128,3584]{1,0:T(8,128)(2,1)S(1)} %pad_maximum_fusion.1), channel_id=1, source_target_pairs={{0,96},{1,97},{2,98},{3,99},{4,100},{5,101},{6,102},{7,103},{8,104... | collective-permute-start | bytes 2752520 | tf_op jit(solution)/shard_map/ppermute | solution.py:739
  64.7 0.0 copy-done.9
  64.8 0.1 pad_maximum_fusion.2
  64.8 0.1 collective-permute-start
  64.9 3.2 %collective-permute-start.2 = (bf16[112,3584]{1,0:T(8,128)(2,1)S(1)}, bf16[112,3584]{1,0:T(8,128)(2,1)}, u32[]{:S(2)}, u32[]{:S(2)}) collective-permute-start(bf16[112,3584]{1,0:T(8,128)(2,1)S(1)} %pad_maximum_fusion.2), channel_id=1, source_target_pairs={{0,96},{1,97},{2,98},{3,99},{4,100},{5,101},{6,102},{7,103},{8,104... | collective-permute-start | bytes 2408456 | tf_op jit(solution)/shard_map/ppermute | solution.py:739
  68.2 54.6 %attend_project.1.y_ref = bf16[32,3584]{1,0:T(8,128)(2,1)} custom-call(bf16[256,4096]{1,0:T(8,128)(2,1)} %copy-done.2, bf16[4096,256]{1,0:T(8,128)(2,1)} %copy-done.3, bf16[128,4096]{1,0:T(8,128)(2,1)} %copy-done.4, f32[8,4096]{1,0:T(8,128)} %copy-done.5, bf16[16384,3584]{1,0:T(8,128)(2,1)} %wo_ref.1), custom_call_target="tpu_custom_call" | custom-call | flops 14000000000 | bytes 70000000 | tf_op jit(solution)/shard_map/attend_project/pallas_call | solution.py:454
  122.8 0.0 copy-done.11
  122.8 0.6 broadcast_in_dim.62.g_ref
  123.4 1.4 pad_maximum_fusion.rest_0_
  124.8 0.0 collective-permute-done.rest_1_
  124.8 0.0 collective-permute-done.2.rest_3_
  124.8 0.0 collective-permute-done.1.rest_2_
  124.8 0.0 copy-start.15
  124.8 0.0 collective-permute-done.3.rest_4_
  124.8 0.9 copy-done.16
  125.7 0.3 copy-done.15
  126.0 78.8 %ffn.1 = bf16[32,3584]{1,0:T(8,128)(2,1)} custom-call(bf16[32,3584]{1,0:T(8,128)(2,1)} %attend_project.1.y_ref, bf16[1,3584]{1,0:T(2,128)(2,1)} %broadcast_in_dim.62.g_ref, bf16[240,3584]{1,0:T(8,128)(2,1)} %pad_maximum_fusion.rest_0_, bf16[112,3584]{1,0:T(8,128)(2,1)} %copy-done.16, bf16[128,3584]{1,0:T(8,128)(2,1)} %copy-done.15, ...), custom_call_target="tpu_custom_call" | custom-call | flops 7000000000 | bytes 14000000 | tf_op jit(solution)/shard_map/ffn/pallas_call | solution.py:694
  204.8 1.6 copy.26
  206.4 0.0 copy-done.1
  (18 shorter events, 0.2 us)
Async XLA Ops:
  0.0 0.9 copy-start
  0.0 5.1 %copy-start.12 = (bf16[768]{0:T(1024)(128)(2,1)S(1)}, bf16[768]{0:T(1024)(128)(2,1)}, u32[]{:S(2)}) copy-start(bf16[768]{0:T(1024)(128)(2,1)} %param.17) | copy-start | bytes 4612
  0.0 5.3 %copy-start.6 = (bf16[3584,576]{0,1:T(8,128)(2,1)S(1)}, bf16[3584,576]{0,1:T(8,128)(2,1)}, u32[]{:S(2)}) copy-start(bf16[3584,576]{0,1:T(8,128)(2,1)} %param.19) | copy-start | bytes 12386308
  5.1 1.5 copy-start.14
  5.1 3.0 %copy-start.13 = (bf16[512]{0:T(512)(128)(2,1)S(1)}, bf16[512]{0:T(512)(128)(2,1)}, u32[]{:S(2)}) copy-start(bf16[512]{0:T(512)(128)(2,1)} %param.20) | copy-start | bytes 3076
  5.2 5.3 %copy-start.10 = (bf16[32,768]{1,0:T(8,128)(2,1)}, bf16[32,768]{1,0:T(8,128)(2,1)S(1)}, u32[]{:S(2)}) copy-start(bf16[32,768]{1,0:T(8,128)(2,1)S(1)} %multiply_convert_fusion) | copy-start | bytes 147460
  5.2 5.3 %copy-start.7 = (bf16[3584,72]{0,1:T(8,128)(2,1)S(1)}, bf16[3584,72]{0,1:T(8,128)(2,1)}, u32[]{:S(2)}) copy-start(bf16[3584,72]{0,1:T(8,128)(2,1)} %param.25) | copy-start | bytes 1548292
  5.3 5.3 %copy-start.8 = (bf16[72,3584]{1,0:T(8,128)(2,1)S(1)}, bf16[72,3584]{1,0:T(8,128)(2,1)}, u32[]{:S(2)}) copy-start(bf16[72,3584]{1,0:T(8,128)(2,1)} %param.26) | copy-start | bytes 1548292
  10.6 0.7 slice-start
  11.4 53.3 %copy-start.9 = (bf16[3584,72]{0,1:T(8,128)(2,1)S(1)}, bf16[3584,72]{0,1:T(8,128)(2,1)}, u32[]{:S(2)}) copy-start(bf16[3584,72]{0,1:T(8,128)(2,1)} %param.24) | copy-start | bytes 1548292
  57.2 1.3 copy-start.2
  58.6 1.3 copy-start.3
  59.9 1.0 copy-start.4
  60.8 0.7 copy-start.5
  61.5 63.3 %collective-permute-start.1 = (bf16[128,3584]{1,0:T(8,128)(2,1)S(1)}, bf16[128,3584]{1,0:T(8,128)(2,1)S(1)}, u32[]{:S(2)}, u32[]{:S(2)}) collective-permute-start(bf16[128,3584]{1,0:T(8,128)(2,1)S(1)} %pad_maximum_fusion.1), channel_id=1, source_target_pairs={{0,32},{1,33},{2,34},{3,35},{4,36},{5,37},{6,38},{7,39},{8,40},{9,... | collective-permute-start | bytes 2752520 | tf_op jit(solution)/shard_map/ppermute | solution.py:739
  61.5 63.3 %collective-permute-start.3 = (bf16[128,3584]{1,0:T(8,128)(2,1)S(1)}, bf16[128,3584]{1,0:T(8,128)(2,1)}, u32[]{:S(2)}, u32[]{:S(2)}) collective-permute-start(bf16[128,3584]{1,0:T(8,128)(2,1)S(1)} %pad_maximum_fusion.1), channel_id=1, source_target_pairs={{0,96},{1,97},{2,98},{3,99},{4,100},{5,101},{6,102},{7,103},{8,104... | collective-permute-start | bytes 2752520 | tf_op jit(solution)/shard_map/ppermute | solution.py:739
  64.8 59.9 %collective-permute-start = (bf16[112,3584]{1,0:T(8,128)(2,1)S(1)}, bf16[112,3584]{1,0:T(8,128)(2,1)S(1)}, u32[]{:S(2)}, u32[]{:S(2)}) collective-permute-start(bf16[112,3584]{1,0:T(8,128)(2,1)S(1)} %pad_maximum_fusion.2), channel_id=1, source_target_pairs={{0,32},{1,33},{2,34},{3,35},{4,36},{5,37},{6,38},{7,39},{8,40},{9,... | collective-permute-start | bytes 2408456 | tf_op jit(solution)/shard_map/ppermute | solution.py:739
  64.9 59.9 %collective-permute-start.2 = (bf16[112,3584]{1,0:T(8,128)(2,1)S(1)}, bf16[112,3584]{1,0:T(8,128)(2,1)}, u32[]{:S(2)}, u32[]{:S(2)}) collective-permute-start(bf16[112,3584]{1,0:T(8,128)(2,1)S(1)} %pad_maximum_fusion.2), channel_id=1, source_target_pairs={{0,96},{1,97},{2,98},{3,99},{4,100},{5,101},{6,102},{7,103},{8,104... | collective-permute-start | bytes 2408456 | tf_op jit(solution)/shard_map/ppermute | solution.py:739
  68.1 54.7 %copy-start.11 = (bf16[3584]{0:T(1024)(128)(2,1)S(1)}, bf16[3584]{0:T(1024)(128)(2,1)}, u32[]{:S(2)}) copy-start(bf16[3584]{0:T(1024)(128)(2,1)} %param.23) | copy-start | bytes 21508
  124.8 0.9 copy-start.16
  124.8 1.2 copy-start.15
  126.0 80.5 %copy-start.1 = (bf16[32,3584]{1,0:T(8,128)(2,1)S(1)}, bf16[32,3584]{1,0:T(8,128)(2,1)}, u32[]{:S(2)}) copy-start(bf16[32,3584]{1,0:T(8,128)(2,1)} %param.14) | copy-start | bytes 688132

commit v3 on v2

--- a/solution.py
+++ b/solution.py
@@ -42,10 +42,10 @@
     return jnp.concatenate([lo_half * cosine - hi_half * sine_v, hi_half * cosine + lo_half * sine_v], axis=-1)
 
 
-GATHER_ORDERS = (("x", "y", "z"), ("y", "z", "x"), ("z", "x", "y"))
-
-
-def gather_kernel_copies(bufs, coord, send_sem, recv_sem, fill_own):
+GATHER_ORDERS = (("z", "x", "y"), ("z", "y", "x"))
+
+
+def gather_kernel_copies(bufs, coord, send_sem, recv_sem, fill_own, on_z_free, on_plane):
     core = coord["core"]
 
     def device(**moved):
@@ -111,6 +111,7 @@
         send(p, "af-", down[a], rows=slice(half, 2 * half), **{a: step(a, 1)})
         along_b(p, -1)
         along_b(p, 1)
+    on_z_free(up["z"], down["z"])
     for p in pieces:
         copies[p]["af+"].wait_recv()
         copies[p]["af-"].wait_recv()
@@ -136,6 +137,12 @@
         for da in (1, 2):
             copies[p][("bf-", da)].wait_recv()
         along_d(p, 2)
+    def whole_plane(dd):
+        for db in order:
+            copies[0][("p", db, dd)].wait_recv()
+        on_plane(step(GATHER_ORDERS[0][2], dd))
+
+    whole_plane(0)
     for db in order:
         for p in pieces:
             a, b, d = GATHER_ORDERS[p]
@@ -147,11 +154,14 @@
             if db in (1, 2):
                 send(p, ("df-", db), down[d], **{a: None, b: step(b, db), d: step(d, 1)})
             to_partner(p, db, 1)
+    whole_plane(-1)
+    whole_plane(1)
     for db in order:
         for p in pieces:
             copies[p][("df+" if db in (0, -1) else "df-", db)].wait_recv()
             to_partner(p, db, 2)
-    for p in pieces:
+    whole_plane(2)
+    for p in pieces[1:]:
         for db in order:
             for dd in order:
                 copies[p][("p", db, dd)].wait_recv()
@@ -173,53 +183,68 @@
     }
 
 
-def qkv_kernel(kv_own, qa_own, qb_own, wqa, wqb, wk, wv, inv_freq, pick, qt_out, k_out, vt_out, pos_out,
-               kv_buf, qa_buf, qb_buf, send_sem, recv_sem, *, blk):
+def qkv_kernel(kv_own, q_own, wq, wk, wv, inv_freq, pick, w_own, qt_out, k_out, vt_out, pos_out, w_left, w_right,
+               kv_buf, q_buf, trig, send_sem, recv_sem, w_sem, *, blk):
     coord = my_coord()
 
     def fill_own():
         at = (coord["z"], coord["y"], coord["x"], coord["core"])
         kv_buf[at] = kv_own[...]
-        qa_buf[at] = qa_own[...]
-        qb_buf[at] = qb_own[...]
-
-    gather_kernel_copies((kv_buf, qa_buf, qb_buf), coord, send_sem, recv_sem, fill_own)
+        q_buf[at] = q_own[...]
 
     nt = (((1,), (1,)), ((), ()))
     half = ROPE_DIM // 2
-    tok_blk = kv_own.shape[0]
-    shards = blk // tok_blk
-    lines = shards // (RING * CORES)
-    n_blk = qt_out.shape[1] // blk
+    f32, bf16 = jnp.float32, jnp.bfloat16
+    row_tok = RING * CORES * kv_own.shape[0]
+    w_copies = []
+
+    def send_weights(up, down):
+        for n, (dst, dev) in enumerate(((w_left, up), (w_right, down))):
+            cp = pltpu.make_async_remote_copy(
+                src_ref=w_own, dst_ref=dst, send_sem=w_sem.at[0, n], recv_sem=w_sem.at[1, n],
+                device_id=dev, device_id_type=pl.DeviceIdType.MESH)
+            cp.start()
+            w_copies.append(cp)
+
+    def keys_values(y):
+        @pl.loop(0, RING)
+        def _(z):
+            lat = kv_buf[z, y].reshape(row_tok, kv_own.shape[1])
+            tail = lat[:, KV_LATENT:]
+            lat = lat[:, :KV_LATENT]
+            rows = pl.ds(pl.multiple_of((z * RING + y) * row_tok, row_tok), row_tok)
+            k_out[rows, :NOPE_DIM] = jnp.dot(lat, wk[...], preferred_element_type=f32).astype(bf16)
+            k_out[rows, NOPE_DIM:] = tail
+            vt_out[:, rows] = lax.dot_general(wv[...], lat, nt, preferred_element_type=f32).astype(bf16)
+            pos = lax.dot_general(pick[...], tail, nt, preferred_element_type=f32)
+            pos_out[:, rows] = pos
+            angle = inv_freq[...] * pos[0:1]
+            trig[:half, rows] = jnp.cos(angle)
+            trig[half:, rows] = jnp.sin(angle)
+
+    gather_kernel_copies((kv_buf, q_buf), coord, send_sem, recv_sem, fill_own, send_weights, keys_values)
+
+    lines = blk // row_tok
     per_z = RING // lines
-    f32, bf16 = jnp.float32, jnp.bfloat16
-
-    @pl.loop(0, n_blk)
+
+    @pl.loop(0, qt_out.shape[1] // blk)
     def _(n):
         at = (n // per_z, pl.ds(lax.rem(n, per_z) * lines, lines))
-        flat = lambda v: v.reshape(blk, v.shape[-1])
-        lat = flat(kv_buf[at])
-        qa = flat(qa_buf[at])
-        qb = flat(qb_buf[at])
-        tail = qb[:, qb.shape[1] - NOPE_DIM:]
+        lat = q_buf[at].reshape(blk, q_own.shape[1])
         rows = pl.ds(pl.multiple_of(n * blk, blk), blk)
-        k_out[rows, :NOPE_DIM] = jnp.dot(lat, wk[...], preferred_element_type=f32).astype(bf16)
-        k_out[rows, NOPE_DIM:] = tail
-        vt_out[:, rows] = lax.dot_general(wv[...], lat, nt, preferred_element_type=f32).astype(bf16)
-        pos = lax.dot_general(pick[...], tail, nt, preferred_element_type=f32)
-        pos_out[:, rows] = pos
-        angle = inv_freq[...] * pos[0:1]
-        cosine, sine = jnp.cos(angle), jnp.sin(angle)
-        qt = lax.dot_general(wqa[...], qa, nt, preferred_element_type=f32)
-        qt += lax.dot_general(wqb[...], qb[:, :qb.shape[1] - NOPE_DIM], nt, preferred_element_type=f32)
+        cosine, sine = trig[:half, rows], trig[half:, rows]
+        qt = lax.dot_general(wq[...], lat, nt, preferred_element_type=f32)
         lo, hi = qt[NOPE_DIM:NOPE_DIM + half], qt[NOPE_DIM + half:]
         qt_out[:NOPE_DIM, rows] = qt[:NOPE_DIM].astype(bf16)
         qt_out[NOPE_DIM:NOPE_DIM + half, rows] = (lo * cosine - hi * sine).astype(bf16)
         qt_out[NOPE_DIM + half:QK_DIM, rows] = (hi * cosine + lo * sine).astype(bf16)
         qt_out[QK_DIM:, rows] = jnp.zeros((2 * NOPE_DIM - QK_DIM, blk), bf16)
 
-
-def gather_qkv(kv_own, qa_own, qb_own, w_uq, w_ukv, tok_total, blk):
+    for cp in w_copies:
+        cp.wait()
+
+
+def gather_qkv(kv_own, q_own, w_uq, w_ukv, w_own, tok_total, blk):
     rows = kv_own.shape[0]
     f32, bf16 = jnp.float32, jnp.bfloat16
     half = ROPE_DIM // 2
@@ -227,7 +252,8 @@
     lane = jnp.arange(NOPE_DIM)[None, :]
     pick = jnp.where(jnp.arange(8)[:, None] == 0, jnp.where(lane == ROPE_DIM, 64.0, jnp.where(lane == ROPE_DIM + 1, 1.0, 0.0)), 0.0).astype(bf16)
     vm = pl.BlockSpec(memory_space=pltpu.VMEM)
-    wa = qa_own.shape[1]
+    hbm = pl.BlockSpec(memory_space=pl.ANY)
+    n_p = len(GATHER_ORDERS)
     buf = lambda own: pltpu.VMEM((RING, RING, RING, CORES, rows, own.shape[1]), bf16)
     return pl.pallas_call(
         functools.partial(qkv_kernel, blk=blk),
@@ -237,24 +263,29 @@
             jax.ShapeDtypeStruct((tok_total, 2 * NOPE_DIM), bf16),
             jax.ShapeDtypeStruct((VALUE_DIM, tok_total), bf16),
             jax.ShapeDtypeStruct((8, tok_total), f32),
+            jax.ShapeDtypeStruct(w_own.shape, bf16),
+            jax.ShapeDtypeStruct(w_own.shape, bf16),
         ),
-        in_specs=[vm] * 9,
-        out_specs=(vm,) * 4,
+        in_specs=[vm] * 7 + [hbm],
+        out_specs=(vm,) * 4 + (hbm,) * 2,
         scratch_shapes=[
-            buf(kv_own), buf(qa_own), buf(qb_own),
-            pltpu.SemaphoreType.DMA((3, GATHER_COPIES)),
-            pltpu.SemaphoreType.DMA((3, GATHER_COPIES)),
+            buf(kv_own), buf(q_own),
+            pltpu.VMEM((ROPE_DIM, tok_total), f32),
+            pltpu.SemaphoreType.DMA((n_p, GATHER_COPIES)),
+            pltpu.SemaphoreType.DMA((n_p, GATHER_COPIES)),
+            pltpu.SemaphoreType.DMA((2, 2)),
         ],
         cost_estimate=pl.CostEstimate(flops=4_000_000_000, bytes_accessed=6_000_000, transcendentals=0),
         compiler_params=pltpu.CompilerParams(collective_id=2, has_side_effects=True, vmem_limit_bytes=40 << 20),
-    )(kv_own, qa_own, qb_own, w_uq[:wa].T, w_uq[wa:].T, w_ukv[:, :NOPE_DIM], w_ukv[:, NOPE_DIM:].T, inv_freq[:, None], pick)
+    )(kv_own, q_own, w_uq.T, w_ukv[:, :NOPE_DIM], w_ukv[:, NOPE_DIM:].T, inv_freq[:, None], pick, w_own)
 
 
 SUB_KEYS = 32
-
-
-def attend_kernel(q_ref, k_ref, v_ref, pos_ref, wo_ref, y_ref, s_even, s_odd, p_even, p_odd, acc_o, stats, o_buf, o_all, w_buf, acc, y_half, y_in,
-                  w_sem, send_sem, recv_sem, fwd_send, fwd_recv, y_sem, *, blk, n_buf):
+FAR_EVERY = 4
+
+
+def attend_kernel(q_ref, k_ref, v_ref, pos_ref, wo_ref, w_left, w_right, y_ref, w_far, s_even, s_odd, p_even, p_odd, acc_o, stats, o_buf, o_all, w_buf, acc, y_half, y_in,
+                  w_sem, send_sem, recv_sem, fwd_send, fwd_recv, y_sem, far_sem, *, blk, n_buf):
     coord = my_coord()
     core, x, y, z = (coord[a] for a in ("core", "x", "y", "z"))
     y_top, y_low = y // 2, lax.rem(y, 2)
@@ -289,6 +320,27 @@
     me_chip = (z * RING + y) * RING + x
     my_line = z * RING + y
     partner = {"sp": me_chip * CORES + 1 - core}
+
+    far_rows = 16
+    far_n = w_far.shape[0] // far_rows
+    far_cut = far_n // 2
+    z_up = {"sp": lax.rem(me_chip + lines, n_chips) * CORES + core}
+    z_dn = {"sp": lax.rem(me_chip + n_chips - lines, n_chips) * CORES + core}
+
+    def far_copy(src, n, dev):
+        rows = pl.ds(pl.multiple_of(n * far_rows, far_rows), far_rows)
+        return pltpu.make_async_remote_copy(
+            src_ref=src.at[rows, :], dst_ref=w_far.at[rows, :], send_sem=far_sem.at[0], recv_sem=far_sem.at[1],
+            device_id=dev, device_id_type=mesh_id)
+
+    def far_step(n):
+        @pl.when(n < far_cut)
+        def _():
+            far_copy(w_left, n, z_up).start()
+
+        @pl.when(n < far_n - far_cut)
+        def _():
+            far_copy(w_right, far_cut + n, z_dn).start()
 
     barrier = pltpu.get_barrier_semaphore()
     pl.semaphore_signal(barrier, inc=1, device_id=partner, device_id_type=mesh_id)
@@ -369,6 +421,10 @@
         def _():
             send_block(i_done)
 
+        @pl.when(lax.rem(t, FAR_EVERY) == 0)
+        def _():
+            far_step(t // FAR_EVERY)
+
         done = (t >= 2) & (t < n_pairs + 2) & (j_c == i_c)
 
         @pl.when(done)
@@ -440,9 +496,11 @@
 
     everything = o_buf.at[pl.ds(0, (n_chips - 1) * chip_rows), :]
     pltpu.make_async_copy(everything, everything, send_sem).wait()
-
-
-def attend_project(qt, k, vt, pos_rows, w_o, blk, group_size, n_buf):
+    pltpu.make_async_copy(w_far, w_far, far_sem.at[0]).wait()
+    pltpu.make_async_copy(w_far, w_far, far_sem.at[1]).wait()
+
+
+def attend_project(qt, k, vt, pos_rows, w_o, w_left, w_right, blk, group_size, n_buf):
     tok = k.shape[0]
     own_rows = tok // group_size
     dim = w_o.shape[1]
@@ -451,12 +509,13 @@
     half = dim // CORES
     f32, bf16 = jnp.float32, jnp.bfloat16
     vm = pl.BlockSpec(memory_space=pltpu.VMEM)
+    hbm = pl.BlockSpec(memory_space=pl.ANY)
     return pl.pallas_call(
         functools.partial(attend_kernel, blk=blk, n_buf=n_buf),
         name="attend_project",
-        out_shape=jax.ShapeDtypeStruct((own_rows, dim), bf16),
-        in_specs=[vm, vm, vm, vm, pl.BlockSpec(memory_space=pl.ANY)],
-        out_specs=vm,
+        out_shape=(jax.ShapeDtypeStruct((own_rows, dim), bf16), jax.ShapeDtypeStruct(w_left.shape, bf16)),
+        in_specs=[vm, vm, vm, vm, hbm, hbm, hbm],
+        out_specs=(vm, hbm),
         scratch_shapes=[
             pltpu.VMEM((blk, blk), f32),
             pltpu.VMEM((blk, blk), f32),
@@ -476,14 +535,15 @@
             pltpu.SemaphoreType.DMA((lines,)),
             pltpu.SemaphoreType.DMA((lines,)),
             pltpu.SemaphoreType.DMA((2,)),
+            pltpu.SemaphoreType.DMA((2,)),
         ],
         cost_estimate=pl.CostEstimate(flops=14_000_000_000, bytes_accessed=70_000_000, transcendentals=9_000_000),
         compiler_params=pltpu.CompilerParams(collective_id=3, has_side_effects=True, vmem_limit_bytes=58 << 20),
-    )(qt, k, vt, pos_rows, w_o)
+    )(qt, k, vt, pos_rows, w_o, w_left, w_right)
 
 
 def ffn_kernel(y_ref, g_ref, *rest, dim, pad, sub, tile_n):
-    n_wt = 5
+    n_wt = 4
     weights = rest[:n_wt]
     (out_ref, ybuf, wgu, wdn, hbuf, gubuf, part, far_l, far_r, in_l, in_r, far2_l, far2_r, in2_l, in2_r,
      w_sem, wx_send, wx_recv, ag_send, ag_recv, rs_send, rs_recv) = rest[n_wt:]
@@ -494,11 +554,11 @@
         return {"sp": ((c["z"] * RING + c["y"]) * RING + c["x"]) * CORES + c["core"]}
 
     x_up, x_dn, y_up, y_dn = device("x", 1), device("x", -1), device("y", 1), device("y", -1)
-    z_up, z_dn, partner = device("z", 1), device("z", -1), device("core", 1)
+    partner = device("core", 1)
     up1, dn1, up2, dn2 = (x_up, y_up), (x_dn, y_dn), (y_up, x_up), (y_dn, x_dn)
 
     barrier = pltpu.get_barrier_semaphore()
-    for nb in (x_up, x_dn, y_up, y_dn, z_up, z_dn, partner):
+    for nb in (x_up, x_dn, y_up, y_dn, partner):
         pl.semaphore_signal(barrier, inc=1, device_id=nb, device_id_type=pl.DeviceIdType.MESH)
 
     w_copies = []
@@ -509,17 +569,11 @@
         w_copies.append(cp)
 
     up0 = 8 * pad
-    own, left_a, left_b, right_a, right_b = weights
-    cut = left_a.shape[0]
-    fetch(own.at[0:pad], wgu.at[0:pad])
-    fetch(own.at[pad:2 * pad], wgu.at[up0:up0 + pad])
-    fetch(own.at[2 * pad:], wdn.at[0:pad])
-    for n, (part_a, part_b) in ((1, (left_a, left_b)), (2, (right_a, right_b))):
+    for n, blk in enumerate(weights):
         r = n * pad
-        fetch(part_a.at[0:pad], wgu.at[r:r + pad])
-        fetch(part_a.at[pad:cut], wgu.at[up0 + r:up0 + r + cut - pad])
-        fetch(part_b.at[0:2 * pad - cut], wgu.at[up0 + r + cut - pad:up0 + r + pad])
-        fetch(part_b.at[2 * pad - cut:], wdn.at[r:r + pad])
+        fetch(blk.at[0:pad], wgu.at[r:r + pad])
+        fetch(blk.at[pad:2 * pad], wgu.at[up0 + r:up0 + r + pad])
+        fetch(blk.at[2 * pad:], wdn.at[r:r + pad])
 
     wx_copies = []
 
@@ -533,7 +587,7 @@
 
     for h in range(2):
         ybuf[h, 0] = y_ref[h * sub:(h + 1) * sub, :]
-    pl.semaphore_wait(barrier, 7)
+    pl.semaphore_wait(barrier, 5)
 
     cols = (slice(0, dim // 2), slice(dim // 2, dim))
     ag_copies = {}
@@ -560,14 +614,9 @@
         ag_send_to(h, 0, 1, dn2[h])
     for cp in w_copies:
         cp.wait()
-    split = cut - pad
-    exchange(wgu, pad, 3 * pad, pad, z_up)
-    exchange(wgu, up0 + pad, up0 + 3 * pad, split, z_up)
-    exchange(wgu, up0 + 2 * pad + split, up0 + 3 * pad + split, pad - split, z_dn)
-    exchange(wdn, 2 * pad, 3 * pad, pad, z_dn)
-    exchange(wgu, 0, 4 * pad, 3 * pad, partner)
-    exchange(wgu, up0, up0 + 4 * pad, 3 * pad, partner)
-    exchange(wdn, 0, 4 * pad, 3 * pad, partner)
+    exchange(wgu, 0, 4 * pad, 4 * pad, partner)
+    exchange(wgu, up0, up0 + 4 * pad, 4 * pad, partner)
+    exchange(wdn, 0, 4 * pad, 4 * pad, partner)
     for h in range(2):
         ag_copies[(h, 3 * RING, None)].wait_recv()
         ag_send_to(h, 3 * RING, far * RING, up1[h], 0)
@@ -589,13 +638,8 @@
         for h in range(2):
             ag_copies[(h, d1 * RING + d2, None)].wait_recv()
 
-    for n in range(4):
-        wx_copies[n].wait_recv()
-    exchange(wgu, 3 * pad, 7 * pad, pad, partner)
-    exchange(wgu, up0 + 3 * pad, up0 + 7 * pad, pad, partner)
-    exchange(wdn, 3 * pad, 7 * pad, pad, partner)
-    for n in range(4, 10):
-        wx_copies[n].wait_recv()
+    for cp in wx_copies:
+        cp.wait_recv()
 
     rows = 2 * RING * sub
     nt = (((1,), (1,)), ((), ()))
@@ -695,7 +739,7 @@
         functools.partial(ffn_kernel, dim=dim, pad=pad, sub=sub, tile_n=256 if (16 * pad) % 256 == 0 else 16 * pad),
         name="ffn",
         out_shape=jax.ShapeDtypeStruct((rows, dim), bf16),
-        in_specs=[vm, vm] + [hbm] * 5,
+        in_specs=[vm, vm] + [hbm] * 4,
         out_specs=vm,
         scratch_shapes=[
             pltpu.VMEM((2, RING * RING, sub, dim), bf16),
@@ -712,9 +756,9 @@
             pltpu.VMEM((2, sub, half), f32),
             pltpu.VMEM((2, sub, dim), f32),
             pltpu.VMEM((2, sub, dim), f32),
-            pltpu.SemaphoreType.DMA((11,)),
-            pltpu.SemaphoreType.DMA((10,)),
-            pltpu.SemaphoreType.DMA((10,)),
+            pltpu.SemaphoreType.DMA((12,)),
+            pltpu.SemaphoreType.DMA((3,)),
+            pltpu.SemaphoreType.DMA((3,)),
             pltpu.SemaphoreType.DMA((32,)),
             pltpu.SemaphoreType.DMA((2, RING * RING + 1)),
             pltpu.SemaphoreType.DMA((40,)),
@@ -732,13 +776,6 @@
     return jnp.concatenate([wide(w_gate.T), wide(w_up.T), wide(w_down)], axis=0), pad
 
 
-def from_z_neighbours(block, group_size):
-    plane = RING * RING * CORES
-    up = [(d, (d + plane) % group_size) for d in range(group_size)]
-    down = [(d, (d - plane) % group_size) for d in range(group_size)]
-    return lax.ppermute(block, 'sp', up), lax.ppermute(block, 'sp', down)
-
-
 def solution(mesh):
     group_size = mesh.shape['sp']
     tok_spec = P(('dp', 'sp'), None)
@@ -750,8 +787,6 @@
         blk_len = x_blk.shape[0]
         tok_total = blk_len * group_size
         w_own, pad = weight_block(w_gate, w_up, w_down)
-        cut = pad + (pad // 2) // 16 * 16
-        left_a, right_a = from_z_neighbours(w_own[:cut], group_size)
 
         q_lin = jnp.dot(x_blk, w_dq, preferred_element_type=jnp.float32)
         c_q = rms_norm(q_lin, g_q).astype(jnp.bfloat16)
@@ -761,13 +796,10 @@
         pos_hi = (pos_blk // 64).astype(jnp.bfloat16)[:, None]
         pos_lo = (pos_blk % 64).astype(jnp.bfloat16)[:, None]
         spare = jnp.zeros((blk_len, NOPE_DIM - ROPE_DIM - 2), jnp.bfloat16)
-        split = KV_LATENT
-        q_rest = jnp.concatenate([c_q[:, split:], k_rope, pos_hi, pos_lo, spare], axis=1)
+        kv_blk = jnp.concatenate([c_kv, k_rope, pos_hi, pos_lo, spare], axis=1)
         blk = min(512, tok_total)
-        qt, k, vt, pos_rows = gather_qkv(c_kv, c_q[:, :split], q_rest, w_uq, w_ukv, tok_total, blk)
-        w_late, pos_rows = lax.optimization_barrier((w_own[cut:], pos_rows))
-        left_b, right_b = from_z_neighbours(w_late, group_size)
-        y_att = attend_project(qt, k, vt, pos_rows, w_o, blk, group_size, 11)
-        return ffn(y_att, g_ffn, (w_own, left_a, left_b, right_a, right_b), pad)
+        qt, k, vt, pos_rows, w_left, w_right = gather_qkv(kv_blk, c_q, w_uq, w_ukv, w_own, tok_total, blk)
+        y_att, w_far = attend_project(qt, k, vt, pos_rows, w_o, w_left, w_right, blk, group_size, 11)
+        return ffn(y_att, g_ffn, (w_own, w_left, w_right, w_far), pad)
 
     return jax.shard_map(device_fn, mesh=mesh, in_specs=(tok_spec, row_spec, row_spec, full_spec, full_spec, col_spec, full_spec, full_spec, col_spec, full_spec, full_spec, col_spec, col_spec, P('sp', None)), out_specs=tok_spec, check_vma=False)

time: 208 us -> 196 us (0.942)
  starting transfers between devices: 6.54 us -> 0 us
  Pallas kernels: 179 us -> 173 us
    pallas_call x1, Pallas kernels: 78.8 us -> 71.6 us  [ffn(): pl.pallas_call(functools.partial(ffn_kernel, dim=dim, pad=pad, sub=sub, t...]
    ppermute x4 -> x0, starting transfers between devices: 6.54 us -> none  [from_z_neighbours(): return (lax.ppermute(block, 'sp', up), lax.ppermute(block, 'sp', down))]
    pallas_call x1, Pallas kernels: 45.8 us -> 49.2 us  [gather_qkv(): pl.pallas_call(functools.partial(qkv_kernel, blk=blk), name='gather_qkv',...]
    slice x5 -> x0, local copies, waits for them, and re-layouts: 2.44 us -> none  [the longest x1 1.14 us: gather_qkv(): w_uq[:wa]]
    dot_general x1, matrix products: 1.26 us -> 3.43 us  [device_fn(): kv_lin = jnp.dot(x_blk, w_dkv, preferred_element_type=jnp.float32)]
    pallas_call x1, Pallas kernels: 54.6 us -> 52.6 us  [attend_project(): pl.pallas_call(functools.partial(attend_kernel, blk=blk, n_buf=n_buf), na...]
    unnamed x38 -> x33, local copies, waits for them, and re-layouts: 8.36 us -> 9.62 us
  transfers between devices with their start and end apart: 4 -> 0, of which waited for: 0 -> 0; matrix products, arithmetic and copies ran while one was open for 1% -> 0% of each run, Pallas kernels for 26% -> 0%
where the time goes in v3:
time: 196 us
  Pallas kernels  173 us (88%)
  local copies, waits for them, and re-layouts  13.3 us (7%)
  matrix products  7.14 us (4%)
    pallas_call x1, Pallas kernels, ffn(): pl.pallas_call(functools.partial(ffn_kernel, dim=dim, pad=pad, sub=sub, t...  71.6 us
    pallas_call x1, Pallas kernels, attend_project(): pl.pallas_call(functools.partial(attend_kernel, blk=blk, n_buf=n_buf), na...  52.6 us
    pallas_call x1, Pallas kernels, gather_qkv(): pl.pallas_call(functools.partial(qkv_kernel, blk=blk), name='gather_qkv',...  49.2 us
    unnamed x33, local copies, waits for them, and re-layouts  9.62 us

profile of v3, /device:TPU:0, one launch (start us, length us, event | category | flops | bytes accessed | tf_op | source)
XLA Modules:
  0.0 195.7 jit_solution(6532196595007425822)
XLA Ops:
  0.0 0.0 copy-start
  0.0 0.0 copy-start.14
  0.0 0.0 copy-start.13
  0.0 0.9 copy-done
  0.9 3.4 %fusion.16 = f32[32,576]{1,0:T(8,128)S(1)} fusion(bf16[32,3584]{1,0:T(8,128)(2,1)S(1)} %copy-done, bf16[3584,576]{0,1:T(8,128)(2,1)} %param.19), kind=kOutput, calls=%fused_computation.43 | convolution fusion | flops 132120576 | bytes 4431872 | tf_op jit(solution)/shard_map/dot_general | solution.py:793
  4.4 0.0 copy-done.14
  4.4 0.1 fusion.13
  4.6 0.1 multiply_reduce_fusion.1
  4.7 0.0 copy-done.13
  4.7 0.0 copy-start.12
  4.7 0.1 multiply_convert_fusion.1
  4.8 0.1 copy.14
  4.9 0.1 copy.15
  5.0 0.0 copy-start.9
  5.0 0.0 copy-start.10
  5.0 0.1 concatenate.9.kv_own
  5.1 1.1 constant_dynamic-slice_fusion.1
  6.2 0.1 copy.22
  6.3 3.7 %multiply_reduce_fusion = (f32[32]{0:T(128)S(1)}, f32[32,768]{1,0:T(8,128)S(1)}) fusion(bf16[32,3584]{1,0:T(8,128)(2,1)S(1)} %copy-done, bf16[3584,768]{1,0:T(8,128)(2,1)} %param.16), kind=kOutput, calls=%fused_computation.11 | convolution fusion | flops 176209888 | bytes 5832832 | tf_op jit(solution)/shard_map/dot_general | solution.py:791
  10.1 0.0 copy-done.12
  10.1 0.1 multiply_convert_fusion.q_own
  10.2 0.0 copy-done.9
  10.2 0.0 copy-done.10
  10.2 1.2 fusion.5.w_own.rest_0_
  11.4 0.0 copy-start.6
  11.4 1.7 constant_dynamic-slice_fusion.2
  13.1 0.2 copy.19
  13.3 0.1 select_convert_fusion.pick
  13.4 49.2 %gather_qkv.1 = (bf16[256,4096]{1,0:T(8,128)(2,1)S(1)}, bf16[4096,256]{1,0:T(8,128)(2,1)S(1)}, bf16[128,4096]{1,0:T(8,128)(2,1)S(1)}, f32[8,4096]{1,0:T(8,128)S(...) custom-call(bf16[32,640]{1,0:T(8,128)(2,1)S(1)} %concatenate.9.kv_own, ...), custom_call_target="tpu_custom_call" | custom-call | flops 4000000000 | bytes 6000000 | tf_op jit(solution)/shard_map/gather_qkv/pallas_call | solution.py:258
  62.5 0.0 copy-done.6
  62.5 0.0 copy-start.2
  62.6 1.3 copy-done.2
  63.9 0.0 copy-start.3
  63.9 1.3 copy-done.3
  65.2 0.0 copy-start.4
  65.2 1.2 copy-done.4
  66.4 0.0 copy-start.5
  66.4 1.3 copy-done.5
  67.7 0.0 copy-start.7
  67.7 1.0 copy-done.7
  68.6 0.0 copy-start.8
  68.6 0.7 copy-done.8
  69.3 0.0 copy-start.11
  69.3 52.6 %attend_project.1 = (bf16[32,3584]{1,0:T(8,128)(2,1)}, bf16[240,3584]{1,0:T(8,128)(2,1)}) custom-call(bf16[256,4096]{1,0:T(8,128)(2,1)} %copy-done.2, bf16[4096,256]{1,0:T(8,128)(2,1)} %copy-done.3, bf16[128,4096]{1,0:T(8,128)(2,1)} %copy-done.7, f32[8,4096]{1,0:T(8,128)} %copy-done.8, bf16[16384,3584]{1,0:T(8,128)(2,1)} %wo_ref.1, ...), custom_call_target="tpu_custom_call" | custom-call | flops 14000000000 | bytes 70000000 | tf_op jit(solution)/shard_map/attend_project/pallas_call | solution.py:513
  121.9 0.0 copy-done.11
  121.9 0.6 broadcast_in_dim.62.g_ref
  122.5 0.0 copy-start.1
  122.5 71.6 %ffn.1 = bf16[32,3584]{1,0:T(8,128)(2,1)} custom-call(bf16[32,3584]{1,0:T(8,128)(2,1)} %get-tuple-element.19.y_ref, bf16[1,3584]{1,0:T(2,128)(2,1)} %broadcast_in_dim.62.g_ref, bf16[240,3584]{1,0:T(8,128)(2,1)} %copy-done.6, bf16[240,3584]{1,0:T(8,128)(2,1)} %copy-done.4, bf16[240,3584]{1,0:T(8,128)(2,1)} %copy-done.5, ...), custom_call_target="tpu_custom_call" | custom-call | flops 7000000000 | bytes 14000000 | tf_op jit(solution)/shard_map/ffn/pallas_call | solution.py:738
  194.1 1.6 copy.24
  195.7 0.0 copy-done.1
  (10 shorter events, 0.1 us)
Async XLA Ops:
  0.0 0.9 copy-start
  0.0 4.4 %copy-start.14 = (s32[32]{0:T(128)S(1)}, s32[32]{0:T(128)}, u32[]{:S(2)}) copy-start(s32[32]{0:T(128)} %param.15) | copy-start | bytes 388
  0.0 4.7 %copy-start.13 = (bf16[512]{0:T(512)(128)(2,1)S(1)}, bf16[512]{0:T(512)(128)(2,1)}, u32[]{:S(2)}) copy-start(bf16[512]{0:T(512)(128)(2,1)} %param.20) | copy-start | bytes 3076
  4.7 5.3 %copy-start.12 = (bf16[768]{0:T(1024)(128)(2,1)S(1)}, bf16[768]{0:T(1024)(128)(2,1)}, u32[]{:S(2)}) copy-start(bf16[768]{0:T(1024)(128)(2,1)} %param.17) | copy-start | bytes 4612
  5.0 5.1 %copy-start.9 = (bf16[72,3584]{1,0:T(8,128)(2,1)S(1)}, bf16[72,3584]{1,0:T(8,128)(2,1)}, u32[]{:S(2)}) copy-start(bf16[72,3584]{1,0:T(8,128)(2,1)} %param.26) | copy-start | bytes 1548292
  5.0 5.1 %copy-start.10 = (bf16[3584,72]{0,1:T(8,128)(2,1)S(1)}, bf16[3584,72]{0,1:T(8,128)(2,1)}, u32[]{:S(2)}) copy-start(bf16[3584,72]{0,1:T(8,128)(2,1)} %param.25) | copy-start | bytes 1548292
  11.4 51.2 %copy-start.6 = (bf16[240,3584]{1,0:T(8,128)(2,1)}, bf16[240,3584]{1,0:T(8,128)(2,1)S(1)}, u32[]{:S(2)}) copy-start(bf16[240,3584]{1,0:T(8,128)(2,1)S(1)} %fusion.5.w_own.rest_0_) | copy-start | bytes 5160964
  62.5 1.3 copy-start.2
  63.9 1.3 copy-start.3
  65.2 1.2 copy-start.4
  66.4 1.3 copy-start.5
  67.7 1.0 copy-start.7
  68.6 0.7 copy-start.8
  69.3 52.6 %copy-start.11 = (bf16[3584]{0:T(1024)(128)(2,1)S(1)}, bf16[3584]{0:T(1024)(128)(2,1)}, u32[]{:S(2)}) copy-start(bf16[3584]{0:T(1024)(128)(2,1)} %param.23) | copy-start | bytes 21508
  122.5 73.2 %copy-start.1 = (bf16[32,3584]{1,0:T(8,128)(2,1)S(1)}, bf16[32,3584]{1,0:T(8,128)(2,1)}, u32[]{:S(2)}) copy-start(bf16[32,3584]{1,0:T(8,128)(2,1)} %param.14) | copy-start | bytes 688132

commit v4 on v3

--- a/solution.py
+++ b/solution.py
@@ -26,26 +26,10 @@
     return vec_in * lax.rsqrt(mean_sq + 1e-6) * gain_vec.astype(jnp.float32)
 
 
-def rope_angles(positions):
-    half_dim = ROPE_DIM // 2
-    inv_freq = 10000.0 ** (-jnp.arange(half_dim, dtype=jnp.float32) / half_dim)
-    return positions.astype(jnp.float32)[..., None] * inv_freq
-
-
-def apply_rope(vec_in, positions):
-    half_dim = ROPE_DIM // 2
-    angles = rope_angles(positions)
-    cosine = jnp.cos(angles)
-    sine_v = jnp.sin(angles)
-    lo_half = vec_in[..., :half_dim]
-    hi_half = vec_in[..., half_dim:]
-    return jnp.concatenate([lo_half * cosine - hi_half * sine_v, hi_half * cosine + lo_half * sine_v], axis=-1)
-
-
 GATHER_ORDERS = (("z", "x", "y"), ("z", "y", "x"))
 
 
-def gather_kernel_copies(bufs, coord, send_sem, recv_sem, fill_own, on_z_free, on_plane):
+def gather_latents(bufs, coord, send_sem, recv_sem, on_z_free, on_plane):
     core = coord["core"]
 
     def device(**moved):
@@ -58,13 +42,6 @@
     up = {a: device(**{a: step(a, 1)}) for a in "xyz"}
     down = {a: device(**{a: step(a, -1)}) for a in "xyz"}
     partner = device(core=1 - core)
-
-    barrier = pltpu.get_barrier_semaphore()
-    for nb in list(up.values()) + list(down.values()) + [partner]:
-        pl.semaphore_signal(barrier, inc=1, device_id=nb, device_id_type=pl.DeviceIdType.MESH)
-    fill_own()
-    pl.semaphore_wait(barrier, 7)
-
     copies = [{} for _ in bufs]
 
     def send(p, key, dev, rows=None, **at):
@@ -111,7 +88,7 @@
         send(p, "af-", down[a], rows=slice(half, 2 * half), **{a: step(a, 1)})
         along_b(p, -1)
         along_b(p, 1)
-    on_z_free(up["z"], down["z"])
+    on_z_free()
     for p in pieces:
         copies[p]["af+"].wait_recv()
         copies[p]["af-"].wait_recv()
@@ -183,111 +160,20 @@
     }
 
 
-def qkv_kernel(kv_own, q_own, wq, wk, wv, inv_freq, pick, w_own, qt_out, k_out, vt_out, pos_out, w_left, w_right,
-               kv_buf, q_buf, trig, send_sem, recv_sem, w_sem, *, blk):
-    coord = my_coord()
-
-    def fill_own():
-        at = (coord["z"], coord["y"], coord["x"], coord["core"])
-        kv_buf[at] = kv_own[...]
-        q_buf[at] = q_own[...]
-
-    nt = (((1,), (1,)), ((), ()))
-    half = ROPE_DIM // 2
-    f32, bf16 = jnp.float32, jnp.bfloat16
-    row_tok = RING * CORES * kv_own.shape[0]
-    w_copies = []
-
-    def send_weights(up, down):
-        for n, (dst, dev) in enumerate(((w_left, up), (w_right, down))):
-            cp = pltpu.make_async_remote_copy(
-                src_ref=w_own, dst_ref=dst, send_sem=w_sem.at[0, n], recv_sem=w_sem.at[1, n],
-                device_id=dev, device_id_type=pl.DeviceIdType.MESH)
-            cp.start()
-            w_copies.append(cp)
-
-    def keys_values(y):
-        @pl.loop(0, RING)
-        def _(z):
-            lat = kv_buf[z, y].reshape(row_tok, kv_own.shape[1])
-            tail = lat[:, KV_LATENT:]
-            lat = lat[:, :KV_LATENT]
-            rows = pl.ds(pl.multiple_of((z * RING + y) * row_tok, row_tok), row_tok)
-            k_out[rows, :NOPE_DIM] = jnp.dot(lat, wk[...], preferred_element_type=f32).astype(bf16)
-            k_out[rows, NOPE_DIM:] = tail
-            vt_out[:, rows] = lax.dot_general(wv[...], lat, nt, preferred_element_type=f32).astype(bf16)
-            pos = lax.dot_general(pick[...], tail, nt, preferred_element_type=f32)
-            pos_out[:, rows] = pos
-            angle = inv_freq[...] * pos[0:1]
-            trig[:half, rows] = jnp.cos(angle)
-            trig[half:, rows] = jnp.sin(angle)
-
-    gather_kernel_copies((kv_buf, q_buf), coord, send_sem, recv_sem, fill_own, send_weights, keys_values)
-
-    lines = blk // row_tok
-    per_z = RING // lines
-
-    @pl.loop(0, qt_out.shape[1] // blk)
-    def _(n):
-        at = (n // per_z, pl.ds(lax.rem(n, per_z) * lines, lines))
-        lat = q_buf[at].reshape(blk, q_own.shape[1])
-        rows = pl.ds(pl.multiple_of(n * blk, blk), blk)
-        cosine, sine = trig[:half, rows], trig[half:, rows]
-        qt = lax.dot_general(wq[...], lat, nt, preferred_element_type=f32)
-        lo, hi = qt[NOPE_DIM:NOPE_DIM + half], qt[NOPE_DIM + half:]
-        qt_out[:NOPE_DIM, rows] = qt[:NOPE_DIM].astype(bf16)
-        qt_out[NOPE_DIM:NOPE_DIM + half, rows] = (lo * cosine - hi * sine).astype(bf16)
-        qt_out[NOPE_DIM + half:QK_DIM, rows] = (hi * cosine + lo * sine).astype(bf16)
-        qt_out[QK_DIM:, rows] = jnp.zeros((2 * NOPE_DIM - QK_DIM, blk), bf16)
-
-    for cp in w_copies:
-        cp.wait()
-
-
-def gather_qkv(kv_own, q_own, w_uq, w_ukv, w_own, tok_total, blk):
-    rows = kv_own.shape[0]
-    f32, bf16 = jnp.float32, jnp.bfloat16
-    half = ROPE_DIM // 2
-    inv_freq = 10000.0 ** (-jnp.arange(half, dtype=f32) / half)
-    lane = jnp.arange(NOPE_DIM)[None, :]
-    pick = jnp.where(jnp.arange(8)[:, None] == 0, jnp.where(lane == ROPE_DIM, 64.0, jnp.where(lane == ROPE_DIM + 1, 1.0, 0.0)), 0.0).astype(bf16)
-    vm = pl.BlockSpec(memory_space=pltpu.VMEM)
-    hbm = pl.BlockSpec(memory_space=pl.ANY)
-    n_p = len(GATHER_ORDERS)
-    buf = lambda own: pltpu.VMEM((RING, RING, RING, CORES, rows, own.shape[1]), bf16)
-    return pl.pallas_call(
-        functools.partial(qkv_kernel, blk=blk),
-        name="gather_qkv",
-        out_shape=(
-            jax.ShapeDtypeStruct((2 * NOPE_DIM, tok_total), bf16),
-            jax.ShapeDtypeStruct((tok_total, 2 * NOPE_DIM), bf16),
-            jax.ShapeDtypeStruct((VALUE_DIM, tok_total), bf16),
-            jax.ShapeDtypeStruct((8, tok_total), f32),
-            jax.ShapeDtypeStruct(w_own.shape, bf16),
-            jax.ShapeDtypeStruct(w_own.shape, bf16),
-        ),
-        in_specs=[vm] * 7 + [hbm],
-        out_specs=(vm,) * 4 + (hbm,) * 2,
-        scratch_shapes=[
-            buf(kv_own), buf(q_own),
-            pltpu.VMEM((ROPE_DIM, tok_total), f32),
-            pltpu.SemaphoreType.DMA((n_p, GATHER_COPIES)),
-            pltpu.SemaphoreType.DMA((n_p, GATHER_COPIES)),
-            pltpu.SemaphoreType.DMA((2, 2)),
-        ],
-        cost_estimate=pl.CostEstimate(flops=4_000_000_000, bytes_accessed=6_000_000, transcendentals=0),
-        compiler_params=pltpu.CompilerParams(collective_id=2, has_side_effects=True, vmem_limit_bytes=40 << 20),
-    )(kv_own, q_own, w_uq.T, w_ukv[:, :NOPE_DIM], w_ukv[:, NOPE_DIM:].T, inv_freq[:, None], pick, w_own)
-
-
 SUB_KEYS = 32
-FAR_EVERY = 4
-
-
-def attend_kernel(q_ref, k_ref, v_ref, pos_ref, wo_ref, w_left, w_right, y_ref, w_far, s_even, s_odd, p_even, p_odd, acc_o, stats, o_buf, o_all, w_buf, acc, y_half, y_in,
-                  w_sem, send_sem, recv_sem, fwd_send, fwd_recv, y_sem, far_sem, *, blk, n_buf):
+LATENT_PARTS = 4
+WEIGHT_HEAD = 32
+
+
+def attend_kernel(x_ref, pos_own, w_dq, g_q, w_dkv, g_kv, w_uq, w_ukv, lane_freq, inv_freq, pick, wo_ref, w_own,
+                  y_ref, w_left, w_right, w_far,
+                  kv_buf, q_buf, trig, q_ref, k_ref, v_ref, pos_ref, dq_buf, dkv_buf, kv_lin, wq_win, wkv_win, wq, wv,
+                  s_even, s_odd, p_even, p_odd, acc_o, stats, o_buf, o_all, w_buf, acc, y_half, y_in,
+                  lat_sem, head_sem, g_send, g_recv, block_sem, w_sem, send_sem, recv_sem, fwd_send, fwd_recv, y_sem,
+                  *, blk, n_buf):
     coord = my_coord()
     core, x, y, z = (coord[a] for a in ("core", "x", "y", "z"))
+    me = lax.axis_index("sp")
     y_top, y_low = y // 2, lax.rem(y, 2)
     lines = RING * RING
     n_chips = lines * RING
@@ -299,6 +185,99 @@
     per_z = n_blk // RING
     f32, bf16, i32 = jnp.float32, jnp.bfloat16, jnp.int32
     scale = SCORE_SCALE * LOG2E
+    nt = (((1,), (1,)), ((), ()))
+    half = ROPE_DIM // 2
+    own_tok, dim = x_ref.shape
+    part_rows = dim // LATENT_PARTS
+
+    def lat_copies(n):
+        rows = pl.ds(n * part_rows, part_rows)
+        return (pltpu.make_async_copy(w_dq.at[rows, :], dq_buf.at[n % 2], lat_sem.at[0, n % 2]),
+                pltpu.make_async_copy(w_dkv.at[:, rows], dkv_buf.at[n % 2], lat_sem.at[1, n % 2]))
+
+    for n in range(2):
+        for cp in lat_copies(n):
+            cp.start()
+    wide_q = wq_win.shape[1]
+    head_copies = (
+        pltpu.make_async_copy(w_uq.at[:, pl.ds(pl.multiple_of(me * QK_DIM - core * (wide_q - QK_DIM), 128), wide_q)], wq_win, head_sem.at[0]),
+        pltpu.make_async_copy(w_ukv.at[:, pl.ds(pl.multiple_of(me * KV_DIM, 128), KV_DIM)], wkv_win, head_sem.at[1]))
+    for cp in head_copies:
+        cp.start()
+
+    me_chip = (z * RING + y) * RING + x
+    my_line = z * RING + y
+    partner = {"sp": me_chip * CORES + 1 - core}
+    z_up = {"sp": lax.rem(me_chip + lines, n_chips) * CORES + core}
+    z_dn = {"sp": lax.rem(me_chip + n_chips - lines, n_chips) * CORES + core}
+
+    barrier = pltpu.get_barrier_semaphore()
+    pl.semaphore_signal(barrier, inc=1, device_id=partner, device_id_type=mesh_id)
+
+    @pl.loop(1, n_chips)
+    def _(n):
+        to = {"sp": lax.rem(me_chip + n, n_chips) * CORES + core}
+        pl.semaphore_signal(barrier, inc=1, device_id=to, device_id_type=mesh_id)
+
+    for ref in (s_even, s_odd, p_even, p_odd):
+        ref[...] = jnp.zeros_like(ref)
+    acc_o[...] = jnp.zeros_like(acc_o)
+    stats[...] = jnp.zeros_like(stats)
+    acc[...] = jnp.zeros_like(acc)
+    kv_lin[...] = jnp.zeros_like(kv_lin)
+    pl.semaphore_wait(barrier, n_chips)
+
+    total_rows = w_own.shape[0]
+    cut = total_rows * 7 // 15
+    block_copies = {}
+
+    def send_rows(key, src, dst, lo, hi, dev):
+        n = len(block_copies)
+        cp = pltpu.make_async_remote_copy(
+            src_ref=src.at[lo:hi], dst_ref=dst.at[lo:hi], send_sem=block_sem.at[0, n], recv_sem=block_sem.at[1, n],
+            device_id=dev, device_id_type=mesh_id)
+        cp.start()
+        block_copies[key] = cp
+
+    send_rows("l0", w_own, w_left, 0, WEIGHT_HEAD, z_up)
+    send_rows("r0", w_own, w_right, cut, cut + WEIGHT_HEAD, z_dn)
+
+    def send_blocks():
+        send_rows("l1", w_own, w_left, WEIGHT_HEAD, cut, z_up)
+        send_rows("r1", w_own, w_right, cut + WEIGHT_HEAD, total_rows, z_dn)
+        send_rows("l2", w_own, w_left, cut, total_rows, z_up)
+        send_rows("r2", w_own, w_right, 0, cut, z_dn)
+
+    def pass_on():
+        for key in ("l0", "l1", "r0", "r1"):
+            block_copies[key].wait_recv()
+        send_rows("f0", w_left, w_far, 0, cut, z_up)
+        send_rows("f1", w_right, w_far, cut, total_rows, z_dn)
+
+    q_lin = jnp.zeros((own_tok, dq_buf.shape[2]), f32)
+    kv_sum = jnp.zeros((own_tok, dkv_buf.shape[1]), f32)
+    for n in range(LATENT_PARTS):
+        for cp in lat_copies(n):
+            cp.wait()
+        x_part = x_ref[:, n * part_rows:(n + 1) * part_rows]
+        q_lin = q_lin + jnp.dot(x_part, dq_buf[n % 2], preferred_element_type=f32)
+        kv_sum = kv_sum + lax.dot_general(x_part, dkv_buf[n % 2], nt, preferred_element_type=f32)
+        if n + 2 < LATENT_PARTS:
+            for cp in lat_copies(n + 2):
+                cp.start()
+    here = (z, y, x, core)
+    q_buf[here] = rms_norm(q_lin, g_q[...]).astype(bf16)
+    kv_buf[here + (slice(None), slice(0, KV_LATENT))] = rms_norm(kv_sum[:, :KV_LATENT], g_kv[...]).astype(bf16)
+    kv_lin[:, :KV_LATENT + ROPE_DIM] = kv_sum
+    turn = kv_lin[:, KV_LATENT:]
+    lane = lax.broadcasted_iota(i32, turn.shape, 1)
+    pos_f = pos_own[...].astype(f32)
+    angle = pos_f * lane_freq[...]
+    other = jnp.where(lane < half, -pltpu.roll(turn, turn.shape[1] - half, 1), pltpu.roll(turn, half, 1))
+    turned = turn * jnp.cos(angle) + other * jnp.sin(angle)
+    pos_hi = jnp.floor(pos_f * (1.0 / 64.0))
+    tail = jnp.where(lane < ROPE_DIM, turned, jnp.where(lane == ROPE_DIM, pos_hi, jnp.where(lane == ROPE_DIM + 1, pos_f - 64.0 * pos_hi, 0.0)))
+    kv_buf[here + (slice(None), slice(KV_LATENT, None))] = tail.astype(bf16)
 
     def line_of(n):
         step = n // 2
@@ -313,49 +292,58 @@
         slot = lax.rem(n, n_buf)
         return pltpu.make_async_copy(wo_ref.at[rows, side], w_buf.at[slot], w_sem.at[slot])
 
-    @pl.loop(0, n_buf)
+    def head_weights():
+        for cp in head_copies:
+            cp.wait()
+        turned_w = wq_win[...].astype(f32).T
+        low, high = turned_w[:QK_DIM], turned_w[wide_q - QK_DIM:]
+        wq[...] = jnp.where(core == 0, low, high).astype(bf16)
+        wv[...] = wkv_win[:, NOPE_DIM:].astype(f32).T.astype(bf16)
+
+        @pl.loop(0, n_buf)
+        def _(n):
+            w_copy(n).start()
+
+    row_tok = RING * CORES * own_tok
+
+    def keys_values(yy):
+        @pl.loop(0, RING)
+        def _(zz):
+            lat = kv_buf[zz, yy].reshape(row_tok, kv_buf.shape[5])
+            tail = lat[:, KV_LATENT:]
+            lat = lat[:, :KV_LATENT]
+            rows = pl.ds(pl.multiple_of((zz * RING + yy) * row_tok, row_tok), row_tok)
+            k_ref[rows, :NOPE_DIM] = jnp.dot(lat, wkv_win[:, :NOPE_DIM], preferred_element_type=f32).astype(bf16)
+            k_ref[rows, NOPE_DIM:] = tail
+            v_ref[:, rows] = lax.dot_general(wv[...], lat, nt, preferred_element_type=f32).astype(bf16)
+            pos = lax.dot_general(pick[...], tail, nt, preferred_element_type=f32)
+            pos_ref[:, rows] = pos
+            angle = inv_freq[...] * pos[0:1]
+            trig[:half, rows] = jnp.cos(angle)
+            trig[half:, rows] = jnp.sin(angle)
+
+    def on_z_free():
+        send_blocks()
+        head_weights()
+
+    gather_latents((kv_buf, q_buf), coord, g_send, g_recv, on_z_free, keys_values)
+    pass_on()
+
+    lines_per_blk = blk // row_tok
+    steps_z = RING // lines_per_blk
+
+    @pl.loop(0, n_blk)
     def _(n):
-        w_copy(n).start()
-
-    me_chip = (z * RING + y) * RING + x
-    my_line = z * RING + y
-    partner = {"sp": me_chip * CORES + 1 - core}
-
-    far_rows = 16
-    far_n = w_far.shape[0] // far_rows
-    far_cut = far_n // 2
-    z_up = {"sp": lax.rem(me_chip + lines, n_chips) * CORES + core}
-    z_dn = {"sp": lax.rem(me_chip + n_chips - lines, n_chips) * CORES + core}
-
-    def far_copy(src, n, dev):
-        rows = pl.ds(pl.multiple_of(n * far_rows, far_rows), far_rows)
-        return pltpu.make_async_remote_copy(
-            src_ref=src.at[rows, :], dst_ref=w_far.at[rows, :], send_sem=far_sem.at[0], recv_sem=far_sem.at[1],
-            device_id=dev, device_id_type=mesh_id)
-
-    def far_step(n):
-        @pl.when(n < far_cut)
-        def _():
-            far_copy(w_left, n, z_up).start()
-
-        @pl.when(n < far_n - far_cut)
-        def _():
-            far_copy(w_right, far_cut + n, z_dn).start()
-
-    barrier = pltpu.get_barrier_semaphore()
-    pl.semaphore_signal(barrier, inc=1, device_id=partner, device_id_type=mesh_id)
-
-    @pl.loop(1, n_chips)
-    def _(n):
-        to = {"sp": lax.rem(me_chip + n, n_chips) * CORES + core}
-        pl.semaphore_signal(barrier, inc=1, device_id=to, device_id_type=mesh_id)
-
-    for ref in (s_even, s_odd, p_even, p_odd):
-        ref[...] = jnp.zeros_like(ref)
-    acc_o[...] = jnp.zeros_like(acc_o)
-    stats[...] = jnp.zeros_like(stats)
-    acc[...] = jnp.zeros_like(acc)
-    pl.semaphore_wait(barrier, n_chips)
+        at = (n // steps_z, pl.ds(lax.rem(n, steps_z) * lines_per_blk, lines_per_blk))
+        lat = q_buf[at].reshape(blk, q_buf.shape[5])
+        rows = pl.ds(pl.multiple_of(n * blk, blk), blk)
+        cosine, sine = trig[:half, rows], trig[half:, rows]
+        qt = lax.dot_general(wq[...], lat, nt, preferred_element_type=f32)
+        lo, hi = qt[NOPE_DIM:NOPE_DIM + half], qt[NOPE_DIM + half:]
+        q_ref[:NOPE_DIM, rows] = qt[:NOPE_DIM].astype(bf16)
+        q_ref[NOPE_DIM:NOPE_DIM + half, rows] = (lo * cosine - hi * sine).astype(bf16)
+        q_ref[NOPE_DIM + half:QK_DIM, rows] = (hi * cosine + lo * sine).astype(bf16)
+        q_ref[QK_DIM:, rows] = jnp.zeros((2 * NOPE_DIM - QK_DIM, blk), bf16)
 
     chips_per_blk = blk // chip_rows
 
@@ -421,10 +409,6 @@
         def _():
             send_block(i_done)
 
-        @pl.when(lax.rem(t, FAR_EVERY) == 0)
-        def _():
-            far_step(t // FAR_EVERY)
-
         done = (t >= 2) & (t < n_pairs + 2) & (j_c == i_c)
 
         @pl.when(done)
@@ -443,6 +427,7 @@
         return (n_next, i_next, j_next), (i_a, j_a), (i_b, j_b), jnp.where(done, i_c, -1)
 
     zero = jnp.int32(0)
+
     def two(u, carry):
         carry = body(2 * u, s_even, s_odd, p_even, p_odd, carry)
         return body(2 * u + 1, s_odd, s_even, p_odd, p_even, carry)
@@ -496,27 +481,53 @@
 
     everything = o_buf.at[pl.ds(0, (n_chips - 1) * chip_rows), :]
     pltpu.make_async_copy(everything, everything, send_sem).wait()
-    pltpu.make_async_copy(w_far, w_far, far_sem.at[0]).wait()
-    pltpu.make_async_copy(w_far, w_far, far_sem.at[1]).wait()
-
-
-def attend_project(qt, k, vt, pos_rows, w_o, w_left, w_right, blk, group_size, n_buf):
-    tok = k.shape[0]
-    own_rows = tok // group_size
-    dim = w_o.shape[1]
+    for key in ("l2", "r2", "f0", "f1"):
+        block_copies[key].wait_recv()
+    for cp in block_copies.values():
+        cp.wait_send()
+
+
+def attend_project(x_blk, pos_blk, w_dq, g_q, w_dkv, g_kv, w_uq, w_ukv, w_o, w_own, blk, group_size, n_buf):
+    own_rows, dim = x_blk.shape
+    tok = own_rows * group_size
     lines = RING * RING
     w_rows = w_o.shape[0] // lines
-    half = dim // CORES
+    side = dim // CORES
     f32, bf16 = jnp.float32, jnp.bfloat16
+    half = ROPE_DIM // 2
+    inv_freq = 10000.0 ** (-jnp.arange(half, dtype=f32) / half)
+    lane = jnp.arange(NOPE_DIM)[None, :]
+    pick = jnp.where(jnp.arange(8)[:, None] == 0, jnp.where(lane == ROPE_DIM, 64.0, jnp.where(lane == ROPE_DIM + 1, 1.0, 0.0)), 0.0).astype(bf16)
+    q_lat = w_dq.shape[1]
+    kv_wide = KV_LATENT + NOPE_DIM
+    part = dim // LATENT_PARTS
+    wide_q = 2 * NOPE_DIM
     vm = pl.BlockSpec(memory_space=pltpu.VMEM)
     hbm = pl.BlockSpec(memory_space=pl.ANY)
+    n_p = len(GATHER_ORDERS)
+    dma = pltpu.SemaphoreType.DMA
+    w_out = jax.ShapeDtypeStruct(w_own.shape, bf16)
     return pl.pallas_call(
         functools.partial(attend_kernel, blk=blk, n_buf=n_buf),
         name="attend_project",
-        out_shape=(jax.ShapeDtypeStruct((own_rows, dim), bf16), jax.ShapeDtypeStruct(w_left.shape, bf16)),
-        in_specs=[vm, vm, vm, vm, hbm, hbm, hbm],
-        out_specs=(vm, hbm),
+        out_shape=(jax.ShapeDtypeStruct((own_rows, dim), bf16), w_out, w_out, w_out),
+        in_specs=[vm, vm, hbm, vm, hbm, vm, hbm, hbm, vm, vm, vm, hbm, hbm],
+        out_specs=(vm, hbm, hbm, hbm),
         scratch_shapes=[
+            pltpu.VMEM((RING, RING, RING, CORES, own_rows, kv_wide), bf16),
+            pltpu.VMEM((RING, RING, RING, CORES, own_rows, q_lat), bf16),
+            pltpu.VMEM((ROPE_DIM, tok), f32),
+            pltpu.VMEM((2 * NOPE_DIM, tok), bf16),
+            pltpu.VMEM((tok, 2 * NOPE_DIM), bf16),
+            pltpu.VMEM((VALUE_DIM, tok), bf16),
+            pltpu.VMEM((8, tok), f32),
+            pltpu.VMEM((2, part, q_lat), bf16),
+            pltpu.VMEM((2, KV_LATENT + ROPE_DIM, part), bf16),
+            pltpu.VMEM((own_rows, kv_wide), f32),
+            pltpu.VMEM((q_lat, wide_q), bf16),
+            pltpu.VMEM((KV_LATENT, KV_DIM), bf16),
+            pltpu.VMEM((QK_DIM, q_lat), bf16),
+            pltpu.VMEM((VALUE_DIM, KV_LATENT), bf16),
             pltpu.VMEM((blk, blk), f32),
             pltpu.VMEM((blk, blk), f32),
             pltpu.VMEM((blk, blk), bf16),
@@ -525,21 +536,19 @@
             pltpu.VMEM((8, blk), f32),
             pltpu.VMEM((tok, VALUE_DIM), bf16),
             pltpu.VMEM((lines, RING, CORES, CORES * own_rows, VALUE_DIM), bf16),
-            pltpu.VMEM((n_buf, w_rows, half), bf16),
-            pltpu.VMEM((CORES * own_rows, half), f32),
-            pltpu.VMEM((CORES * own_rows, half), bf16),
-            pltpu.VMEM((own_rows, half), bf16),
-            pltpu.SemaphoreType.DMA((n_buf,)),
-            pltpu.SemaphoreType.DMA,
-            pltpu.SemaphoreType.DMA((lines,)),
-            pltpu.SemaphoreType.DMA((lines,)),
-            pltpu.SemaphoreType.DMA((lines,)),
-            pltpu.SemaphoreType.DMA((2,)),
-            pltpu.SemaphoreType.DMA((2,)),
+            pltpu.VMEM((n_buf, w_rows, side), bf16),
+            pltpu.VMEM((CORES * own_rows, side), f32),
+            pltpu.VMEM((CORES * own_rows, side), bf16),
+            pltpu.VMEM((own_rows, side), bf16),
+            dma((2, 2)), dma((2,)),
+            dma((n_p, GATHER_COPIES)), dma((n_p, GATHER_COPIES)),
+            dma((2, 8)),
+            dma((n_buf,)), dma, dma((lines,)), dma((lines,)), dma((lines,)), dma((2,)),
         ],
-        cost_estimate=pl.CostEstimate(flops=14_000_000_000, bytes_accessed=70_000_000, transcendentals=9_000_000),
-        compiler_params=pltpu.CompilerParams(collective_id=3, has_side_effects=True, vmem_limit_bytes=58 << 20),
-    )(qt, k, vt, pos_rows, w_o, w_left, w_right)
+        cost_estimate=pl.CostEstimate(flops=18_000_000_000, bytes_accessed=80_000_000, transcendentals=9_000_000),
+        compiler_params=pltpu.CompilerParams(collective_id=3, has_side_effects=True, vmem_limit_bytes=62 << 20),
+    )(x_blk, pos_blk[:, None], w_dq, g_q[None, :], w_dkv.T, g_kv[None, :], w_uq, w_ukv, jnp.tile(inv_freq, NOPE_DIM // half)[None, :],
+      inv_freq[:, None], pick, w_o, w_own)
 
 
 def ffn_kernel(y_ref, g_ref, *rest, dim, pad, sub, tile_n):
@@ -788,18 +797,8 @@
         tok_total = blk_len * group_size
         w_own, pad = weight_block(w_gate, w_up, w_down)
 
-        q_lin = jnp.dot(x_blk, w_dq, preferred_element_type=jnp.float32)
-        c_q = rms_norm(q_lin, g_q).astype(jnp.bfloat16)
-        kv_lin = jnp.dot(x_blk, w_dkv, preferred_element_type=jnp.float32)
-        c_kv = rms_norm(kv_lin[:, :KV_LATENT], g_kv).astype(jnp.bfloat16)
-        k_rope = apply_rope(kv_lin[:, KV_LATENT:], pos_blk).astype(jnp.bfloat16)
-        pos_hi = (pos_blk // 64).astype(jnp.bfloat16)[:, None]
-        pos_lo = (pos_blk % 64).astype(jnp.bfloat16)[:, None]
-        spare = jnp.zeros((blk_len, NOPE_DIM - ROPE_DIM - 2), jnp.bfloat16)
-        kv_blk = jnp.concatenate([c_kv, k_rope, pos_hi, pos_lo, spare], axis=1)
-        blk = min(512, tok_total)
-        qt, k, vt, pos_rows, w_left, w_right = gather_qkv(kv_blk, c_q, w_uq, w_ukv, w_own, tok_total, blk)
-        y_att, w_far = attend_project(qt, k, vt, pos_rows, w_o, w_left, w_right, blk, group_size, 11)
+        y_att, w_left, w_right, w_far = attend_project(
+            x_blk, pos_blk, w_dq, g_q, w_dkv, g_kv, w_uq, w_ukv, w_o, w_own, min(512, tok_total), group_size, 8)
         return ffn(y_att, g_ffn, (w_own, w_left, w_right, w_far), pad)
 
-    return jax.shard_map(device_fn, mesh=mesh, in_specs=(tok_spec, row_spec, row_spec, full_spec, full_spec, col_spec, full_spec, full_spec, col_spec, full_spec, full_spec, col_spec, col_spec, P('sp', None)), out_specs=tok_spec, check_vma=False)
+    return jax.shard_map(device_fn, mesh=mesh, in_specs=(tok_spec, row_spec, row_spec, full_spec, full_spec, full_spec, full_spec, full_spec, full_spec, full_spec, full_spec, col_spec, col_spec, P('sp', None)), out_specs=tok_spec, check_vma=False)

time: 196 us -> 185 us (0.944)
  matrix products: 7.14 us -> 0 us
  local copies, waits for them, and re-layouts: 13.3 us -> 7.49 us
  other arithmetic: 1.74 us -> 3.94 us
    pallas_call x1, Pallas kernels: 52.6 us -> 102 us  [attend_project(): pl.pallas_call(functools.partial(attend_kernel, blk=blk, n_buf=n_buf), na...]
    pallas_call x1 -> x0, Pallas kernels: 49.2 us -> none  [gather_qkv(): pl.pallas_call(functools.partial(qkv_kernel, blk=blk), name='gather_qkv',...]
    unnamed x33 -> x1, local copies, waits for them, and re-layouts: 9.62 us -> 1.64 us
    dot_general x2 -> x0, matrix products: 7.14 us -> none  [the longest x1 3.71 us: device_fn(): q_lin = jnp.dot(x_blk, w_dq, preferred_element_type=jnp.float32)]
    broadcast_in_dim x3, local copies, waits for them, and re-layouts: 0.2 us -> 3.89 us  [the longest x1 1.34 us: attend_project(): pos_blk[:, None]]
where the time goes in v4:
time: 185 us
  Pallas kernels  173 us (94%)
  local copies, waits for them, and re-layouts  7.49 us (4%)
  other arithmetic  3.94 us (2%)
    pallas_call x1, Pallas kernels, attend_project(): pl.pallas_call(functools.partial(attend_kernel, blk=blk, n_buf=n_buf), na...  102 us
    pallas_call x1, Pallas kernels, ffn(): pl.pallas_call(functools.partial(ffn_kernel, dim=dim, pad=pad, sub=sub, t...  71.5 us

profile of v4, /device:TPU:0, one launch (start us, length us, event | category | flops | bytes accessed | tf_op | source)
XLA Modules:
  0.0 184.9 jit_solution(2065396538729097425)
XLA Ops:
  0.0 0.6 select_convert_fusion.pick
  0.7 0.7 broadcast_in_dim_tile.3.lane_freq
  1.3 1.3 broadcast_in_dim.49.g_kv
  2.6 1.3 broadcast_in_dim.48.g_q
  3.9 1.3 broadcast_in_dim.56.g_ref
  5.2 1.3 copy.14.pos_own
  6.5 0.6 multiply_power_fusion.inv_freq
  7.1 2.7 %fusion.5.w_own.rest_0_ = bf16[240,3584]{1,0:T(8,128)(2,1)} fusion(bf16[72,3584]{1,0:T(8,128)(2,1)} %param.26, bf16[72,3584]{1,0:T(8,128)(2,1)} %bitcast.5, bf16[72,3584]{1,0:T(8,128)(2,1)} %bitcast.6), kind=kLoop, calls=%fused_computation.9 | loop fusion | flops 12042240 | bytes 3268608 | tf_op jit(solution)/shard_map/concatenate | solution.py:785
  9.8 101.9 %attend_project.1 = (bf16[32,3584]{1,0:T(8,128)(2,1)}, bf16[240,3584]{1,0:T(8,128)(2,1)}, bf16[240,3584]{1,0:T(8,128)(2,1)}, bf16[240,3584]{1,0:T(8,128)(2,1)}) custom-call(bf16[32,3584]{1,0:T(8,128)(2,1)} %x_ref.1, s32[32,1]{1,0:T(8,128)} %copy.14.pos_own, bf16[3584,768]{1,0:T(8,128)(2,1)} %w_dq.1, bf16[1,768]{1,0:T(2,128)(2,1)} %broadcast_in_dim.48.g_q, ...), custom_call_target="tpu_custom_call" | custom-call | flops 17999998976 | bytes 80000000 | tf_op jit(solution)/shard_map/attend_project/pallas_call | solution.py:510
  111.7 71.5 %ffn.1 = bf16[32,3584]{1,0:T(8,128)(2,1)} custom-call(bf16[32,3584]{1,0:T(8,128)(2,1)} %get-tuple-element.9.y_ref, bf16[1,3584]{1,0:T(2,128)(2,1)} %broadcast_in_dim.56.g_ref, bf16[240,3584]{1,0:T(8,128)(2,1)} %fusion.5.w_own.rest_0_, bf16[240,3584]{1,0:T(8,128)(2,1)} %get-tuple-element.10.rest_1_, bf16[240,3584]{1,0:T(8,128)(2,1)} %get-tuple-element.11.rest_2_, ...), custom_call_target="tpu_custom_call" | custom-call | flops 7000000000 | bytes 14000000 | tf_op jit(solution)/shard_map/ffn/pallas_call | solution.py:747
  183.2 1.6 copy.16
  (4 shorter events, 0.0 us)
